TPU v7x, 128 devices: a whole 4x4x4 slice. The times are simulated.
128 devices in a mesh: gx: 8 (over y, core), gy: 16 (over z, x).
Axes of the slice: x: 4, y: 4, z: 4, core: 2. Of those that a mesh axis runs over, the one named last changes fastest.
Arguments:
- fluid_state: float32 [4, 64, 256, 256], P(None, 'gx', 'gy'), may hold values from -3 to 3
- node_disp: float32 [3, 524288], P(None, ('gx', 'gy')), may hold values from -0.02 to 0.02
- node_vel: float32 [3, 524288], P(None, ('gx', 'gy')), may hold values from -1 to 1
- fiber_angles: float32 [2, 65536], P(None, ('gx', 'gy')), may hold values from -3.140625 to 3.140625
- connectivity: int32 [27, 65536], P(None, ('gx', 'gy')), may hold values from 0 to 4095
- send_blocks: int32 [128, 128, 4], P(('gx', 'gy')), may hold values from 0 to 256, as said below
- interp_slots: int32 [4, 4096], P(None, ('gx', 'gy')), may hold values from 0 to 511, as said below
- weight_index: int32 [4, 4096], P(None, ('gx', 'gy')), may hold values from 0 to 127
- share_nodes: int32 [128, 128, 16], P(('gx', 'gy')), may hold values from 0 to 4096, as said below
- weight_table: bfloat16 [128, 128, 128], replicated, may hold values from -0.25 to 0.25
Outputs:
- fluid_out: float32 [4, 64, 256, 256], P(None, 'gx', 'gy')
- disp_out: float32 [3, 524288], P(None, ('gx', 'gy'))
- vel_out: float32 [3, 524288], P(None, ('gx', 'gy'))
Inputs may be any that keep to these rules, and one draw needn't show every extreme that they name: `send_blocks`: entry [s, d, j] is the block of tile s in its j-th slot to part d; 256 marks an empty slot; in each [s, d] the filled slots come first, and some [s, d] are full. `interp_slots`: column p * 32 + b names slots of part p's received buffer, counted as source tile times 4 plus slot. `share_nodes`: entry [p, q, j] is the node of part p paired with node [q, p, j] of part q; 4096 marks an unused slot, unused on both sides together; [p, p] holds only unused slots; used slots come first.
All inputs are finite; a program needn't handle non-finite values.
Results may differ from a plain program's by a relative error of at most 0.0046.
Values may be sent and summed in bfloat16 or wider, within the bound.
No kernel may reach another device: no remote copies, remote signals or barrier semaphores. Data moves between devices by JAX's collectives and lax.ppermute only.
A program may use at most 128 MiB of HBM per device.

v0:
```python
import math

import jax
import jax.numpy as jnp
import numpy as np
from jax import lax
from jax.experimental import pallas as pl
from jax.experimental.pallas import tpu as pltpu
from jax.sharding import PartitionSpec as P

STEPS = 3

time_step = 0.1
viscosity = 1.0
sound_square = 1.0
penalty = 4.0
node_mass = 0.5
shear_modulus = 2.0
bulk_modulus = 4.0
fiber_stiff = 2.0
fiber_exponent = 1.0

BF16 = jnp.bfloat16
F32 = jnp.float32
AXES = ("gx", "gy")


def lagrange(degree, position):
    if degree == 0:
        return 0.5 * position * (position - 1.0)
    if degree == 1:
        return 1.0 - position * position
    return 0.5 * position * (position + 1.0)


def slope(degree, position):
    if degree == 0:
        return position - 0.5
    if degree == 1:
        return -2.0 * position
    return position + 0.5


def derivative_matrix():
    points = (-1.0 / math.sqrt(3.0), 1.0 / math.sqrt(3.0))
    table = np.zeros((8, 3, 27))
    for point in range(8):
        coords = (points[point // 4], points[point // 2 % 2], points[point % 2])
        for node in range(27):
            orders = (node // 9, node // 3 % 3, node % 3)
            for direction in range(3):
                value = 2.0
                for axis in range(3):
                    shape = slope if axis == direction else lagrange
                    value = value * shape(orders[axis], coords[axis])
                table[point, direction, node] = value
    table = table.astype(np.float32)
    big = np.zeros((72, 112), np.float32)
    for i in range(3):
        for j in range(3):
            for node in range(27):
                big[(3 * i + j) * 8 : (3 * i + j) * 8 + 8, node * 4 + i] = table[:, j, node]
    return big


def dot(a, b, precision=None):
    return lax.dot_general(
        a, b, (((1,), (0,)), ((), ())), precision=precision, preferred_element_type=F32
    )


def dot_nt(a, b):
    return lax.dot_general(a, b, (((1,), (1,)), ((), ())), preferred_element_type=F32)


def node_onehot(row):
    lane = row & 127
    return jnp.where(lax.broadcasted_iota(jnp.int32, (128, 512), 0) == lane, 1.0, 0.0).astype(BF16)


def node_high(row):
    return jnp.broadcast_to(row >> 7, (8, 512)) - (
        lax.broadcasted_iota(jnp.int32, (8, 512), 0) >> 2
    )


def pick_rows(table, high):
    picked = jnp.where(high == 0, table[0:8], 0.0)
    for r in range(1, 16):
        picked = picked + jnp.where(high == 2 * r, table[8 * r : 8 * r + 8], 0.0)
    return picked + pltpu.roll(picked, 4, 0)


def spread_rows(value, high):
    return jnp.concatenate([jnp.where(high == 2 * r, value, 0.0) for r in range(16)], axis=0)


def both_halves(value, odd):
    turned = pltpu.roll(value, 4, 0)
    low = lax.broadcasted_iota(jnp.int32, value.shape, 0) < 4
    return jnp.where(low, turned, value) if odd else jnp.where(low, value, turned)


def split(value):
    head = value.astype(BF16)
    return head, (value - head.astype(F32)).astype(BF16)


def elastic_kernel(
    disp_ref, idx_ref, fiber_ref, deriv_ref, derivt_ref, elastic_ref, shared_ref,
    nodal_ref, work_ref, turn_ref,
):
    head, tail = split(disp_ref[...])
    both = jnp.concatenate([head, tail], axis=1)

    def fetch(pair, carry):
        halves = []
        for s in range(2):
            row = idx_ref[pl.ds(2 * pair + s, 1), :]
            hot = node_onehot(row)
            table = dot(both, jnp.concatenate([hot, hot], axis=0))
            halves.append(pick_rows(table, node_high(row)))
        low = lax.broadcasted_iota(jnp.int32, (8, 512), 0) < 4
        nodal_ref[pl.ds(pl.multiple_of(8 * pair, 8), 8), :] = jnp.where(low, halves[0], halves[1])
        return carry

    lax.fori_loop(0, 14, fetch, 0)
    work_ref[...] = dot(deriv_ref[...], nodal_ref[...], lax.Precision.HIGHEST)

    def entry(i, j):
        value = work_ref[8 * (3 * i + j) : 8 * (3 * i + j) + 8, :]
        return value + 1.0 if i == j else value

    F = [[entry(i, j) for j in range(3)] for i in range(3)]
    fiber = [fiber_ref[j : j + 1, :] for j in range(3)]

    def cofactor(i, j):
        i1, i2, j1, j2 = (i + 1) % 3, (i + 2) % 3, (j + 1) % 3, (j + 2) % 3
        return F[i1][j1] * F[i2][j2] - F[i1][j2] * F[i2][j1]

    cof = [[cofactor(i, j) for j in range(3)] for i in range(3)]
    volume = F[0][0] * cof[0][0] + F[0][1] * cof[0][1] + F[0][2] * cof[0][2]
    along = [F[i][0] * fiber[0] + F[i][1] * fiber[1] + F[i][2] * fiber[2] for i in range(3)]
    excess = along[0] * along[0] + along[1] * along[1] + along[2] * along[2] - 1.0
    weight = 2.0 * fiber_stiff * excess * jnp.exp(fiber_exponent * excess * excess)
    factor = bulk_modulus * (volume - 1.0) - shear_modulus
    for i in range(3):
        pulled = weight * along[i]
        for j in range(3):
            work_ref[8 * (3 * i + j) : 8 * (3 * i + j) + 8, :] = (
                shear_modulus * F[i][j] + factor * cof[i][j] + pulled * fiber[j]
            )
    nodal_ref[...] = dot(derivt_ref[...], work_ref[...], lax.Precision.HIGHEST)

    def deposit(pair, total):
        rows = nodal_ref[pl.ds(pl.multiple_of(8 * pair, 8), 8), :]
        for s in range(2):
            row = idx_ref[pl.ds(2 * pair + s, 1), :]
            high = node_high(row)
            value = both_halves(rows, s == 1)
            value_head, value_tail = split(value)
            left = jnp.concatenate(
                [
                    spread_rows(value_head.astype(F32), high),
                    spread_rows(value_tail.astype(F32), high),
                ],
                axis=0,
            ).astype(BF16)
            both_parts = dot_nt(left, node_onehot(row))
            total = total + both_parts[:128] + both_parts[128:]
        return total

    elastic = lax.fori_loop(0, 14, deposit, jnp.zeros((128, 128), F32))
    elastic_ref[...] = elastic
    sent = elastic.astype(BF16)
    turn_ref[...] = jnp.zeros((128, 128), F32)
    for t in range(4):
        row = idx_ref[28 + t : 29 + t, :]
        picked = pick_rows(dot(sent, node_onehot(row)), node_high(row))
        for jj in range(4):
            turn_ref[16 * t + 4 * jj : 16 * t + 4 * jj + 4, :] = picked[0:4, 128 * jj : 128 * jj + 128]
    shared_ref[...] = turn_ref[...].T


def couple_kernel(
    windex_ref, recv_ref, vel_ref, pick_ref, pickt_ref, table_ref, shared_ref,
    payload_ref, coupling_ref, rows_ref, chosen_ref, spread_ref,
):
    rows_ref[...] = recv_ref[...].astype(F32)
    chosen_ref[...] = jnp.zeros((512, 128), F32)
    pick = pick_ref[...]
    for q in range(3):
        plane = rows_ref[pl.ds(q, 512, stride=4), :].astype(BF16)
        chosen_ref[pl.ds(q, 128, stride=4), :] = dot(pick, plane)

    def group(g, carry):
        start = pl.multiple_of(16 * g, 16)
        left = jnp.concatenate(
            [chosen_ref[pl.ds(128 * k + start, 16), :] for k in range(4)], axis=1
        ).astype(BF16)
        owner = lax.broadcasted_iota(jnp.int32, (16, 128), 0) >> 2
        weights = []
        sampled = jnp.zeros((16, 128), F32)
        for s in range(4):
            weight = jnp.concatenate(
                [table_ref[windex_ref[32 * k + 4 * g + s]] for k in range(4)], axis=1
            )
            weights.append(weight)
            sampled = jnp.where(owner == s, dot_nt(left, weight), sampled)
        coupling = penalty * (sampled - vel_ref[pl.ds(start, 16), :])
        coupling_ref[pl.ds(start, 16), :] = coupling
        pushed = (-coupling).astype(BF16)
        wide_owner = lax.broadcasted_iota(jnp.int32, (16, 512), 0) >> 2
        out = jnp.zeros((16, 512), F32)
        for s in range(4):
            out = jnp.where(wide_owner == s, dot(pushed, weights[s]), out)
        for k in range(4):
            spread_ref[pl.ds(128 * k + start, 16), :] = out[:, 128 * k : 128 * k + 128]
        return carry

    lax.fori_loop(0, 8, group, 0)
    pickt = pickt_ref[...]
    for q in range(3):
        head, tail = split(spread_ref[pl.ds(q, 128, stride=4), :])
        rows_ref[pl.ds(q, 512, stride=4), :] = dot(pickt, jnp.concatenate([head, tail], axis=0))
    rows_ref[pl.ds(3, 512, stride=4), :] = jnp.zeros((512, 128), F32)
    rows_ref[pl.ds(3, 128, stride=16), :] = shared_ref[...]
    payload_ref[...] = rows_ref[...].astype(BF16)


def write_payload(send, blocks_ref, rows_ref, payload_ref):
    sent = dot(send, blocks_ref[...])
    for q in range(3):
        rows_ref[pl.ds(q, 512, stride=4), :] = sent[:, 128 * q : 128 * q + 128]
    rows_ref[pl.ds(3, 512, stride=4), :] = jnp.zeros((512, 128), F32)
    payload_ref[...] = rows_ref[...].astype(BF16)


def store_blocks(blocks_ref, x, q, plane):
    for half in range(2):
        blocks_ref[128 * half + 16 * x : 128 * half + 16 * x + 16, 128 * q : 128 * q + 128] = plane[
            :, 128 * half : 128 * half + 128
        ].astype(BF16)


def pack_kernel(state_ref, send_ref, payload_ref, blocks_ref, rows_ref):
    for q in range(3):
        for x in range(8):
            store_blocks(blocks_ref, x, q, state_ref[q, x])
    write_payload(send_ref[...], blocks_ref, rows_ref, payload_ref)


def update_kernel(last):
    def kernel(
        recv_ref, state_ref, xlow_ref, xhigh_ref, ylow_ref, yhigh_ref, sendt_ref, send_ref,
        elastic_ref, coupling_ref, vel_ref, disp_ref, share_ref, *rest,
    ):
        if last:
            new_ref, velout_ref, dispout_ref, rows_ref, force_ref, turn_ref = rest
        else:
            (
                new_ref, velout_ref, dispout_ref, payload_ref, xlowout_ref, xhighout_ref,
                ylowout_ref, yhighout_ref, rows_ref, force_ref, turn_ref, blocks_ref,
            ) = rest
        rows_ref[...] = recv_ref[...].astype(F32)
        planes = jnp.concatenate(
            [rows_ref[pl.ds(q, 512, stride=4), :].astype(BF16) for q in range(3)], axis=1
        )
        force_ref[...] = dot(sendt_ref[...], planes)

        turn_ref[...] = rows_ref[pl.ds(3, 128, stride=16), :].T
        total = elastic_ref[...]
        for t in range(4):
            row = share_ref[t : t + 1, :]
            pieces = []
            for jj in range(4):
                first = 16 * t + 8 * (jj // 2)
                pieces.append(both_halves(turn_ref[first : first + 8, :], jj % 2 == 1))
            left = spread_rows(jnp.concatenate(pieces, axis=1), node_high(row)).astype(BF16)
            total = total + dot_nt(left, node_onehot(row))
        velocity = vel_ref[...] + time_step / node_mass * (total + coupling_ref[...])
        velout_ref[...] = velocity
        dispout_ref[...] = disp_ref[...] + time_step * velocity

        yrow = lax.broadcasted_iota(jnp.int32, (16, 256), 0)
        zlane = lax.broadcasted_iota(jnp.int32, (16, 256), 1)

        def around(f, x):
            centre = state_ref[f, x]
            xm = xlow_ref[f] if x == 0 else state_ref[f, x - 1]
            xp = xhigh_ref[f] if x == 7 else state_ref[f, x + 1]
            ym = jnp.where(yrow == 0, ylow_ref[f, x], pltpu.roll(centre, 1, 0))
            yp = jnp.where(yrow == 15, yhigh_ref[f, x], pltpu.roll(centre, 15, 0))
            zm = jnp.where(zlane == 0, 0.0, pltpu.roll(centre, 1, 1))
            zp = jnp.where(zlane == 255, 0.0, pltpu.roll(centre, 255, 1))
            return centre, ((xm, xp), (ym, yp), (zm, zp))

        for x in range(8):
            density, near = around(3, x)
            divergence = jnp.zeros((16, 256), F32)
            for q in range(3):
                centre, pairs = around(q, x)
                laplace = -6.0 * centre
                for below, above in pairs:
                    laplace = laplace + (below + above)
                gradient = 0.5 * (near[q][1] - near[q][0])
                below, above = pairs[q]
                divergence = divergence + 0.5 * (
                    (1.0 + near[q][1]) * above - (1.0 + near[q][0]) * below
                )
                force = jnp.concatenate(
                    [
                        force_ref[128 * h + 16 * x : 128 * h + 16 * x + 16, 128 * q : 128 * q + 128]
                        for h in range(2)
                    ],
                    axis=1,
                )
                fresh = centre + time_step * (
                    viscosity * laplace - sound_square * gradient + force
                )
                new_ref[q, x] = fresh
                if not last:
                    store_blocks(blocks_ref, x, q, fresh)
                    put_edges(q, x, fresh, xlowout_ref, xhighout_ref, ylowout_ref, yhighout_ref)
            fresh = density - time_step * divergence
            new_ref[3, x] = fresh
            if not last:
                put_edges(3, x, fresh, xlowout_ref, xhighout_ref, ylowout_ref, yhighout_ref)
        if not last:
            write_payload(send_ref[...], blocks_ref, rows_ref, payload_ref)

    return kernel


def put_edges(f, x, fresh, xlowout_ref, xhighout_ref, ylowout_ref, yhighout_ref):
    if x == 0:
        xlowout_ref[f] = fresh
    if x == 7:
        xhighout_ref[f] = fresh
    ylowout_ref[f, x] = fresh[0:1]
    yhighout_ref[f, x] = fresh[15:16]


VMEM = pl.BlockSpec(memory_space=pltpu.VMEM)
SMEM = pl.BlockSpec(memory_space=pltpu.SMEM)


def shape(dims, dtype=F32):
    return jax.ShapeDtypeStruct(dims, dtype)


def call(kernel, outs, specs, scratch, flops, name):
    return pl.pallas_call(
        kernel,
        out_shape=outs,
        in_specs=specs,
        out_specs=[VMEM] * len(outs),
        scratch_shapes=scratch,
        cost_estimate=pl.CostEstimate(flops=flops, transcendentals=0, bytes_accessed=2_000_000),
        compiler_params=pltpu.CompilerParams(vmem_limit_bytes=32 * 1024 * 1024),
        name=name,
    )


def exchange(payload):
    return lax.all_to_all(
        payload.reshape(128, 16, 128), AXES, split_axis=0, concat_axis=0, tiled=True
    ).reshape(2048, 128)


def halo(edges):
    xlow, xhigh, ylow, yhigh = edges

    def shift(low, high, axis):
        size = lax.axis_size(axis)
        up = [(i, i + 1) for i in range(size - 1)]
        down = [(b, a) for a, b in up]
        return lax.ppermute(high, axis, up), lax.ppermute(low, axis, down)

    xm, xp = shift(xlow, xhigh, "gx")
    ym, yp = shift(ylow, yhigh, "gy")
    return xm, xp, ym, yp


def to_rows(nodes):
    return jnp.pad(nodes.reshape(3, 32, 128).transpose(1, 0, 2), ((0, 0), (0, 1), (0, 0))).reshape(
        128, 128
    )


def from_rows(rows):
    return rows.reshape(32, 4, 128)[:, :3].transpose(1, 0, 2).reshape(3, 4096)


def body(
    fluid_state, node_disp, node_vel, fiber_angles, connectivity,
    send_blocks, interp_slots, weight_index, share_nodes, weight_table,
):
    big = derivative_matrix()
    deriv = jnp.asarray(big)
    derivt = jnp.asarray(-0.125 * big.T)
    unused = jnp.full((1, 512), 4096, jnp.int32)
    share = share_nodes[0].T.reshape(4, 512)
    index = jnp.concatenate([connectivity, unused, share], axis=0)
    fiber = jnp.stack(
        [
            jnp.cos(fiber_angles[0]) * jnp.cos(fiber_angles[1]),
            jnp.cos(fiber_angles[0]) * jnp.sin(fiber_angles[1]),
            jnp.sin(fiber_angles[0]),
        ]
    )
    sends = send_blocks[0].reshape(512)
    sends = jnp.where(sends < 256, (sends & 1) * 128 + (sends >> 1), -1)
    blocks_range = jnp.arange(256, dtype=jnp.int32)
    slots_range = jnp.arange(512, dtype=jnp.int32)
    send = (sends[:, None] == blocks_range[None, :]).astype(BF16)
    sendt = (blocks_range[:, None] == sends[None, :]).astype(BF16)
    slots = interp_slots.reshape(128)
    pick = (slots[:, None] == slots_range[None, :]).astype(BF16)
    twice = jnp.concatenate([slots, slots])
    pickt = (slots_range[:, None] == twice[None, :]).astype(BF16)
    windex = weight_index.reshape(128)

    elastic_call = call(
        elastic_kernel,
        [shape((128, 128)), shape((128, 128))],
        [VMEM] * 5,
        [pltpu.VMEM((112, 512), F32), pltpu.VMEM((72, 512), F32), pltpu.VMEM((128, 128), F32)],
        3_000_000_000,
        "elastic",
    )
    couple_call = call(
        couple_kernel,
        [shape((2048, 128), BF16), shape((128, 128))],
        [SMEM] + [VMEM] * 6,
        [
            pltpu.VMEM((2048, 128), F32),
            pltpu.VMEM((512, 128), F32),
            pltpu.VMEM((512, 128), F32),
        ],
        1_000_000_000,
        "couple",
    )
    pack_call = call(
        pack_kernel,
        [shape((2048, 128), BF16)],
        [VMEM] * 2,
        [pltpu.VMEM((256, 384), BF16), pltpu.VMEM((2048, 128), F32)],
        200_000_000,
        "pack",
    )

    def update_call(last):
        outs = [shape((4, 8, 16, 256)), shape((128, 128)), shape((128, 128))]
        scratch = [
            pltpu.VMEM((2048, 128), F32),
            pltpu.VMEM((256, 384), F32),
            pltpu.VMEM((128, 128), F32),
        ]
        if not last:
            outs = outs + [
                shape((2048, 128), BF16),
                shape((4, 16, 256)),
                shape((4, 16, 256)),
                shape((4, 8, 1, 256)),
                shape((4, 8, 1, 256)),
            ]
            scratch = scratch + [pltpu.VMEM((256, 384), BF16)]
        return call(
            update_kernel(last), outs, [VMEM] * 13, scratch, 500_000_000,
            "finish" if last else "update",
        )

    state = fluid_state
    displace = to_rows(node_disp)
    velocity = to_rows(node_vel)
    payload = pack_call(state, send)[0]
    edges = (state[:, 0], state[:, 7], state[:, :, 0:1], state[:, :, 15:16])
    for step in range(STEPS):
        last = step == STEPS - 1
        received = exchange(payload)
        around = halo(edges)
        elastic, shared = elastic_call(displace, index, fiber, deriv, derivt)
        outbound, coupling = couple_call(
            windex, received, velocity, pick, pickt, weight_table, shared
        )
        inbound = exchange(outbound)
        results = update_call(last)(
            inbound, state, *around, sendt, send, elastic, coupling, velocity, displace, share
        )
        state, velocity, displace = results[:3]
        if not last:
            payload = results[3]
            edges = results[4:8]
    return (state, from_rows(displace), from_rows(velocity))


def solution(mesh):
    placed = (
        P(None, "gx", "gy", None),
        P(None, AXES),
        P(None, AXES),
        P(None, AXES),
        P(None, AXES),
        P(AXES, None, None),
        P(None, AXES),
        P(None, AXES),
        P(AXES, None, None),
        P(),
    )
    return jax.shard_map(
        body,
        mesh=mesh,
        in_specs=placed,
        out_specs=(P(None, "gx", "gy", None), P(None, AXES), P(None, AXES)),
        check_vma=False,
    )
```

profile of v0, /device:TPU:14, one launch (start us, length us, event | category | flops | bytes accessed | tf_op | source)
XLA Modules:
  0.0 176.9 jit_solution(3159104201409496184)
XLA Ops:
  0.6 0.7 add_select_fusion
  1.7 1.0 copy-done.3
  2.7 1.2 pack.1
  3.9 10.4 %all-to-all-start = ((bf16[128,16,128]{2,1,0:T(8,128)(2,1)}), bf16[128,16,128]{2,1,0:T(8,128)(2,1)S(1)}, u32[]{:S(2)}, u32[]{:S(2)}) async-start(bf16[128,16,128]{2,1,0:T(8,128)(2,1)} %bitcast), calls=%async_computation | async-start | bytes 1048576 | tf_op jit(solution)/shard_map/all_to_all | solution.py:366
  14.3 0.8 eq.57
  15.1 0.9 cosine_multiply_fusion
  16.0 0.7 reshape.125.share_ref
  16.9 0.9 pad_add_fusion.idx_ref
  17.8 0.8 reshape.118.windex_ref
  18.6 0.9 pad.8
  19.4 0.9 pad.7
  20.4 0.8 copy-done.5
  21.2 0.8 copy-done.7
  21.9 9.2 %elastic.3 = (f32[128,128]{1,0:T(8,128)S(1)}, f32[128,128]{1,0:T(8,128)S(1)}) custom-call(f32[128,128]{1,0:T(8,128)S(1)} %bitcast.50, s32[32,512]{1,0:T(8,128)S(1)} %pad_add_fusion.idx_ref, f32[3,512]{1,0:T(4,128)S(1)} %pad_maximum_fusion.fiber_ref, f32[72,112]{1,0:T(8,128)S(1)} %copy-done.7, f32[112,72]{1,0:T(8,128)S(1)} %copy-done.5), custom_call_target="tpu_custom_call" | custom-call | flops 3000000000 | bytes 2000000 | tf_op jit(solution)/shard_map/elastic/pallas_call | solution.py:483
  31.2 2.2 %copy-done = bf16[128,128,128]{2,1,0:T(8,128)(2,1)S(1)} copy-done((bf16[128,128,128]{2,1,0:T(8,128)(2,1)S(1)}, bf16[128,128,128]{2,1,0:T(8,128)(2,1)}, u32[]{:S(2)}) %copy-start) | copy-done | bytes 4194328
  33.4 5.5 %couple.3 = (bf16[2048,128]{1,0:T(8,128)(2,1)}, f32[128,128]{1,0:T(8,128)S(1)}) custom-call(s32[128]{0:T(128)S(1)} %reshape.118.windex_ref, bf16[2048,128]{1,0:T(8,128)(2,1)S(1)} %bitcast.45, f32[128,128]{1,0:T(8,128)S(1)} %bitcast.48, bf16[128,512]{1,0:T(8,128)(2,1)S(1)} %fusion.3.pick_ref, bf16[512,256]{1,0:T(8,128)(2,1)S(1)} %fusion.1.pickt_ref, ...), custom_call_target="tpu_custom_call" | custom-call | flops 1000000000 | bytes 2000000 | tf_op jit(solution)/shard_map/couple/pallas_call | solution.py:484
  38.9 9.8 %all-to-all-start.1 = ((bf16[128,16,128]{2,1,0:T(8,128)(2,1)}), bf16[128,16,128]{2,1,0:T(8,128)(2,1)S(1)}, u32[]{:S(2)}, u32[]{:S(2)}) async-start(bf16[128,16,128]{2,1,0:T(8,128)(2,1)} %bitcast.10), calls=%async_computation.1 | async-start | bytes 1048576 | tf_op jit(solution)/shard_map/all_to_all | solution.py:366
  48.7 2.8 %collective-permute-start.3 = (f32[4,8,1,256]{3,2,1,0:T(1,128)S(1)}, f32[4,8,1,256]{3,2,1,0:T(1,128)S(1)}, u32[]{:S(2)}, u32[]{:S(2)}) collective-permute-start(f32[4,8,1,256]{3,2,1,0:T(1,128)S(1)} %get-tuple-element.65), channel_id=1, source_target_pairs={{1,0},{2,1},{3,2},{4,3},{5,4},{6,5},{7,6},{8,7},{9,8},{10,9},{11,1... | collective-permute-start | bytes 98312 | tf_op jit(solution)/shard_map/ppermute | solution.py:378
  51.5 5.2 %collective-permute-start.2 = (f32[4,8,1,256]{3,2,1,0:T(1,128)S(1)}, f32[4,8,1,256]{3,2,1,0:T(1,128)S(1)}, u32[]{:S(2)}, u32[]{:S(2)}) collective-permute-start(f32[4,8,1,256]{3,2,1,0:T(1,128)S(1)} %get-tuple-element.66), channel_id=1, source_target_pairs={{0,1},{1,2},{2,3},{3,4},{4,5},{5,6},{6,7},{7,8},{8,9},{9,10},{10,1... | collective-permute-start | bytes 98312 | tf_op jit(solution)/shard_map/ppermute | solution.py:378
  56.7 1.9 %collective-permute-start.1 = (f32[4,16,256]{2,1,0:T(8,128)S(1)}, f32[4,16,256]{2,1,0:T(8,128)S(1)}, u32[]{:S(2)}, u32[]{:S(2)}) collective-permute-start(f32[4,16,256]{2,1,0:T(8,128)S(1)} %get-tuple-element.67), channel_id=1, source_target_pairs={{16,0},{32,16},{48,32},{64,48},{80,64},{96,80},{112,96},{17,1},{33... | collective-permute-start | bytes 196616 | tf_op jit(solution)/shard_map/ppermute | solution.py:378
  58.6 2.4 %collective-permute-start = (f32[4,16,256]{2,1,0:T(8,128)S(1)}, f32[4,16,256]{2,1,0:T(8,128)S(1)}, u32[]{:S(2)}, u32[]{:S(2)}) collective-permute-start(f32[4,16,256]{2,1,0:T(8,128)S(1)} %get-tuple-element.68), channel_id=1, source_target_pairs={{0,16},{16,32},{32,48},{48,64},{64,80},{80,96},{96,112},{1,17},{17... | collective-permute-start | bytes 196616 | tf_op jit(solution)/shard_map/ppermute | solution.py:378
  61.1 3.1 %collective-permute-done.xlow_ref = f32[4,16,256]{2,1,0:T(8,128)S(1)} collective-permute-done((f32[4,16,256]{2,1,0:T(8,128)S(1)}, f32[4,16,256]{2,1,0:T(8,128)S(1)}, u32[]{:S(2)}, u32[]{:S(2)}) %collective-permute-start) | collective-permute-done | bytes 65568 | tf_op jit(solution)/shard_map/ppermute | solution.py:378
  64.2 2.0 %update.2 = (f32[4,8,16,256]{3,2,1,0:T(8,128)S(1)}, f32[128,128]{1,0:T(8,128)S(1)}, f32[128,128]{1,0:T(8,128)S(1)}, bf16[2048,128]{1,0:T(8,128)(2,1)}, f32[4,16,...) custom-call(bf16[2048,128]{1,0:T(8,128)(2,1)S(1)} %bitcast.42, ...), custom_call_target="tpu_custom_call" | custom-call | flops 500000000 | bytes 2000000 | tf_op jit(solution)/shard_map/update/pallas_call | solution.py:488
  66.2 9.5 %all-to-all-start.2 = ((bf16[128,16,128]{2,1,0:T(8,128)(2,1)}), bf16[128,16,128]{2,1,0:T(8,128)(2,1)S(1)}, u32[]{:S(2)}, u32[]{:S(2)}) async-start(bf16[128,16,128]{2,1,0:T(8,128)(2,1)} %bitcast.14), calls=%async_computation.2 | async-start | bytes 1048576 | tf_op jit(solution)/shard_map/all_to_all | solution.py:366
  75.8 9.2 %elastic.4 = (f32[128,128]{1,0:T(8,128)S(1)}, f32[128,128]{1,0:T(8,128)S(1)}) custom-call(f32[128,128]{1,0:T(8,128)S(1)} %get-tuple-element.40.disp_ref, s32[32,512]{1,0:T(8,128)S(1)} %pad_add_fusion.idx_ref, f32[3,512]{1,0:T(4,128)S(1)} %pad_maximum_fusion.fiber_ref, f32[72,112]{1,0:T(8,128)S(1)} %copy-done.8, f32[112,72]{1,0:T(8,128)S(1)} %copy-done.6), custom_call_target="tpu_custom_call" | custom-call | flops 3000000000 | bytes 2000000 | tf_op jit(solution)/shard_map/elastic/pallas_call | solution.py:483
  85.0 2.5 %all-to-all-done.2 = bf16[128,16,128]{2,1,0:T(8,128)(2,1)S(1)} async-done(((bf16[128,16,128]{2,1,0:T(8,128)(2,1)}), bf16[128,16,128]{2,1,0:T(8,128)(2,1)S(1)}, u32[]{:S(2)}, u32[]{:S(2)}) %all-to-all-start.2) | async-done | bytes 524320 | tf_op jit(solution)/shard_map/all_to_all | solution.py:366
  87.5 2.2 %copy-done.1 = bf16[128,128,128]{2,1,0:T(8,128)(2,1)S(1)} copy-done((bf16[128,128,128]{2,1,0:T(8,128)(2,1)S(1)}, bf16[128,128,128]{2,1,0:T(8,128)(2,1)}, u32[]{:S(2)}) %copy-start.1) | copy-done | bytes 4194328
  89.7 5.5 %couple.4 = (bf16[2048,128]{1,0:T(8,128)(2,1)}, f32[128,128]{1,0:T(8,128)S(1)}) custom-call(s32[128]{0:T(128)S(1)} %reshape.118.windex_ref, bf16[2048,128]{1,0:T(8,128)(2,1)S(1)} %bitcast.47, f32[128,128]{1,0:T(8,128)S(1)} %get-tuple-element.39.vel_ref, bf16[128,512]{1,0:T(8,128)(2,1)S(1)} %fusion.3.pick_ref, bf16[512,256]{1,0:T(8,128)(2,1)S(1)} %fusion.1.pickt_ref, ...), custom_call_target="tpu_custom_call" | custom-call | flops 1000000000 | bytes 2000000 | tf_op jit(solution)/shard_map/couple/pallas_call | solution.py:484
  95.2 7.3 %all-to-all-start.3 = ((bf16[128,16,128]{2,1,0:T(8,128)(2,1)}), bf16[128,16,128]{2,1,0:T(8,128)(2,1)S(1)}, u32[]{:S(2)}, u32[]{:S(2)}) async-start(bf16[128,16,128]{2,1,0:T(8,128)(2,1)} %bitcast.16), calls=%async_computation.3 | async-start | bytes 1048576 | tf_op jit(solution)/shard_map/all_to_all | solution.py:366
  102.5 2.0 %collective-permute-start.4 = (f32[4,16,256]{2,1,0:T(8,128)S(1)}, f32[4,16,256]{2,1,0:T(8,128)S(1)}, u32[]{:S(2)}, u32[]{:S(2)}) collective-permute-start(f32[4,16,256]{2,1,0:T(8,128)S(1)} %get-tuple-element.44), channel_id=1, source_target_pairs={{0,16},{16,32},{32,48},{48,64},{64,80},{80,96},{96,112},{1,17},{17... | collective-permute-start | bytes 196616 | tf_op jit(solution)/shard_map/ppermute | solution.py:378
  104.5 3.5 %collective-permute-start.5 = (f32[4,16,256]{2,1,0:T(8,128)S(1)}, f32[4,16,256]{2,1,0:T(8,128)S(1)}, u32[]{:S(2)}, u32[]{:S(2)}) collective-permute-start(f32[4,16,256]{2,1,0:T(8,128)S(1)} %get-tuple-element.45), channel_id=1, source_target_pairs={{16,0},{32,16},{48,32},{64,48},{80,64},{96,80},{112,96},{17,1},{33... | collective-permute-start | bytes 196616 | tf_op jit(solution)/shard_map/ppermute | solution.py:378
  108.0 3.6 %collective-permute-start.6 = (f32[4,8,1,256]{3,2,1,0:T(1,128)S(1)}, f32[4,8,1,256]{3,2,1,0:T(1,128)S(1)}, u32[]{:S(2)}, u32[]{:S(2)}) collective-permute-start(f32[4,8,1,256]{3,2,1,0:T(1,128)S(1)} %get-tuple-element.46), channel_id=1, source_target_pairs={{0,1},{1,2},{2,3},{3,4},{4,5},{5,6},{6,7},{7,8},{8,9},{9,10},{10,1... | collective-permute-start | bytes 98312 | tf_op jit(solution)/shard_map/ppermute | solution.py:378
  111.6 2.3 %collective-permute-start.7 = (f32[4,8,1,256]{3,2,1,0:T(1,128)S(1)}, f32[4,8,1,256]{3,2,1,0:T(1,128)S(1)}, u32[]{:S(2)}, u32[]{:S(2)}) collective-permute-start(f32[4,8,1,256]{3,2,1,0:T(1,128)S(1)} %get-tuple-element.47), channel_id=1, source_target_pairs={{1,0},{2,1},{3,2},{4,3},{5,4},{6,5},{7,6},{8,7},{9,8},{10,9},{11,1... | collective-permute-start | bytes 98312 | tf_op jit(solution)/shard_map/ppermute | solution.py:378
  113.9 5.6 %collective-permute-done.7.yhigh_ref = f32[4,8,1,256]{3,2,1,0:T(1,128)S(1)} collective-permute-done((f32[4,8,1,256]{3,2,1,0:T(1,128)S(1)}, f32[4,8,1,256]{3,2,1,0:T(1,128)S(1)}, u32[]{:S(2)}, u32[]{:S(2)}) %collective-permute-start.7) | collective-permute-done | bytes 32800 | tf_op jit(solution)/shard_map/ppermute | solution.py:378
  119.5 2.1 %update.3 = (f32[4,8,16,256]{3,2,1,0:T(8,128)S(1)}, f32[128,128]{1,0:T(8,128)S(1)}, f32[128,128]{1,0:T(8,128)S(1)}, bf16[2048,128]{1,0:T(8,128)(2,1)}, f32[4,16,...) custom-call(bf16[2048,128]{1,0:T(8,128)(2,1)S(1)} %bitcast.43, ...), custom_call_target="tpu_custom_call" | custom-call | flops 500000000 | bytes 2000000 | tf_op jit(solution)/shard_map/update/pallas_call | solution.py:488
  121.6 9.2 %all-to-all-start.4 = ((bf16[128,16,128]{2,1,0:T(8,128)(2,1)}), bf16[128,16,128]{2,1,0:T(8,128)(2,1)S(1)}, u32[]{:S(2)}, u32[]{:S(2)}) async-start(bf16[128,16,128]{2,1,0:T(8,128)(2,1)} %bitcast.18), calls=%async_computation.4 | async-start | bytes 1048576 | tf_op jit(solution)/shard_map/all_to_all | solution.py:366
  130.8 9.2 %elastic.5 = (f32[128,128]{1,0:T(8,128)S(1)}, f32[128,128]{1,0:T(8,128)S(1)}) custom-call(f32[128,128]{1,0:T(8,128)S(1)} %get-tuple-element.52.disp_ref, s32[32,512]{1,0:T(8,128)S(1)} %pad_add_fusion.idx_ref, f32[3,512]{1,0:T(4,128)S(1)} %pad_maximum_fusion.fiber_ref, f32[72,112]{1,0:T(8,128)S(1)} %copy-done.8, f32[112,72]{1,0:T(8,128)S(1)} %copy-done.6), custom_call_target="tpu_custom_call" | custom-call | flops 3000000000 | bytes 2000000 | tf_op jit(solution)/shard_map/elastic/pallas_call | solution.py:483
  140.0 2.5 %all-to-all-done.4 = bf16[128,16,128]{2,1,0:T(8,128)(2,1)S(1)} async-done(((bf16[128,16,128]{2,1,0:T(8,128)(2,1)}), bf16[128,16,128]{2,1,0:T(8,128)(2,1)S(1)}, u32[]{:S(2)}, u32[]{:S(2)}) %all-to-all-start.4) | async-done | bytes 524320 | tf_op jit(solution)/shard_map/all_to_all | solution.py:366
  142.6 2.2 %copy-done.2 = bf16[128,128,128]{2,1,0:T(8,128)(2,1)S(1)} copy-done((bf16[128,128,128]{2,1,0:T(8,128)(2,1)S(1)}, bf16[128,128,128]{2,1,0:T(8,128)(2,1)}, u32[]{:S(2)}) %copy-start.2) | copy-done | bytes 4194328
  144.7 5.5 %couple.5 = (bf16[2048,128]{1,0:T(8,128)(2,1)}, f32[128,128]{1,0:T(8,128)S(1)}) custom-call(s32[128]{0:T(128)S(1)} %reshape.118.windex_ref, bf16[2048,128]{1,0:T(8,128)(2,1)S(1)} %bitcast.46, f32[128,128]{1,0:T(8,128)S(1)} %get-tuple-element.51.vel_ref, bf16[128,512]{1,0:T(8,128)(2,1)S(1)} %fusion.3.pick_ref, bf16[512,256]{1,0:T(8,128)(2,1)S(1)} %fusion.1.pickt_ref, ...), custom_call_target="tpu_custom_call" | custom-call | flops 1000000000 | bytes 2000000 | tf_op jit(solution)/shard_map/couple/pallas_call | solution.py:484
  150.3 7.3 %all-to-all-start.5 = ((bf16[128,16,128]{2,1,0:T(8,128)(2,1)}), bf16[128,16,128]{2,1,0:T(8,128)(2,1)S(1)}, u32[]{:S(2)}, u32[]{:S(2)}) async-start(bf16[128,16,128]{2,1,0:T(8,128)(2,1)} %bitcast.20), calls=%async_computation.5 | async-start | bytes 1048576 | tf_op jit(solution)/shard_map/all_to_all | solution.py:366
  157.5 2.0 %collective-permute-start.8 = (f32[4,16,256]{2,1,0:T(8,128)S(1)}, f32[4,16,256]{2,1,0:T(8,128)S(1)}, u32[]{:S(2)}, u32[]{:S(2)}) collective-permute-start(f32[4,16,256]{2,1,0:T(8,128)S(1)} %get-tuple-element.56), channel_id=1, source_target_pairs={{0,16},{16,32},{32,48},{48,64},{64,80},{80,96},{96,112},{1,17},{17... | collective-permute-start | bytes 196616 | tf_op jit(solution)/shard_map/ppermute | solution.py:378
  159.6 3.5 %collective-permute-start.9 = (f32[4,16,256]{2,1,0:T(8,128)S(1)}, f32[4,16,256]{2,1,0:T(8,128)S(1)}, u32[]{:S(2)}, u32[]{:S(2)}) collective-permute-start(f32[4,16,256]{2,1,0:T(8,128)S(1)} %get-tuple-element.57), channel_id=1, source_target_pairs={{16,0},{32,16},{48,32},{64,48},{80,64},{96,80},{112,96},{17,1},{33... | collective-permute-start | bytes 196616 | tf_op jit(solution)/shard_map/ppermute | solution.py:378
  163.1 3.6 %collective-permute-start.10 = (f32[4,8,1,256]{3,2,1,0:T(1,128)S(1)}, f32[4,8,1,256]{3,2,1,0:T(1,128)S(1)}, u32[]{:S(2)}, u32[]{:S(2)}) collective-permute-start(f32[4,8,1,256]{3,2,1,0:T(1,128)S(1)} %get-tuple-element.58), channel_id=1, source_target_pairs={{0,1},{1,2},{2,3},{3,4},{4,5},{5,6},{6,7},{7,8},{8,9},{9,10},{10,1... | collective-permute-start | bytes 98312 | tf_op jit(solution)/shard_map/ppermute | solution.py:378
  166.7 2.3 %collective-permute-start.11 = (f32[4,8,1,256]{3,2,1,0:T(1,128)S(1)}, f32[4,8,1,256]{3,2,1,0:T(1,128)S(1)}, u32[]{:S(2)}, u32[]{:S(2)}) collective-permute-start(f32[4,8,1,256]{3,2,1,0:T(1,128)S(1)} %get-tuple-element.59), channel_id=1, source_target_pairs={{1,0},{2,1},{3,2},{4,3},{5,4},{6,5},{7,6},{8,7},{9,8},{10,9},{11,1... | collective-permute-start | bytes 98312 | tf_op jit(solution)/shard_map/ppermute | solution.py:378
  169.0 5.6 %collective-permute-done.11.yhigh_ref = f32[4,8,1,256]{3,2,1,0:T(1,128)S(1)} collective-permute-done((f32[4,8,1,256]{3,2,1,0:T(1,128)S(1)}, f32[4,8,1,256]{3,2,1,0:T(1,128)S(1)}, u32[]{:S(2)}, u32[]{:S(2)}) %collective-permute-start.11) | collective-permute-done | bytes 32800 | tf_op jit(solution)/shard_map/ppermute | solution.py:378
  174.6 1.6 finish.1
  176.2 0.7 slice_bitcast_fusion
  (36 shorter events, 0.8 us)
Async XLA Ops:
  1.7 1.0 copy-start.3
  3.9 27.2 %all-to-all-start = ((bf16[128,16,128]{2,1,0:T(8,128)(2,1)}), bf16[128,16,128]{2,1,0:T(8,128)(2,1)S(1)}, u32[]{:S(2)}, u32[]{:S(2)}) async-start(bf16[128,16,128]{2,1,0:T(8,128)(2,1)} %bitcast), calls=%async_computation | async-start | bytes 1048576 | tf_op jit(solution)/shard_map/all_to_all | solution.py:366
  20.3 0.8 copy-start.5
  21.2 0.8 copy-start.7
  21.9 26.7 %copy-start.4 = (f32[4,8,16,256]{3,2,1,0:T(8,128)S(1)}, f32[4,8,16,256]{3,2,1,0:T(8,128)}, u32[]{:S(2)}) copy-start(f32[4,8,16,256]{3,2,1,0:T(8,128)} %state_ref.3) | copy-start | bytes 1572868
  31.2 2.2 %copy-start = (bf16[128,128,128]{2,1,0:T(8,128)(2,1)S(1)}, bf16[128,128,128]{2,1,0:T(8,128)(2,1)}, u32[]{:S(2)}) copy-start(bf16[128,128,128]{2,1,0:T(8,128)(2,1)} %table_ref.5) | copy-start | bytes 12582916
  33.4 42.4 %copy-start.6 = (f32[112,72]{1,0:T(8,128)S(1)}, f32[112,72]{1,0:T(8,128)}, u32[]{:S(2)}) copy-start(f32[112,72]{1,0:T(8,128)} %constant.18.clone.derivt_ref) | copy-start | bytes 96772
  33.4 42.4 %copy-start.8 = (f32[72,112]{1,0:T(8,128)S(1)}, f32[72,112]{1,0:T(8,128)}, u32[]{:S(2)}) copy-start(f32[72,112]{1,0:T(8,128)} %constant.17.clone.deriv_ref) | copy-start | bytes 96772
  38.9 25.3 %all-to-all-start.1 = ((bf16[128,16,128]{2,1,0:T(8,128)(2,1)}), bf16[128,16,128]{2,1,0:T(8,128)(2,1)S(1)}, u32[]{:S(2)}, u32[]{:S(2)}) async-start(bf16[128,16,128]{2,1,0:T(8,128)(2,1)} %bitcast.10), calls=%async_computation.1 | async-start | bytes 1048576 | tf_op jit(solution)/shard_map/all_to_all | solution.py:366
  48.7 12.4 %collective-permute-start.3 = (f32[4,8,1,256]{3,2,1,0:T(1,128)S(1)}, f32[4,8,1,256]{3,2,1,0:T(1,128)S(1)}, u32[]{:S(2)}, u32[]{:S(2)}) collective-permute-start(f32[4,8,1,256]{3,2,1,0:T(1,128)S(1)} %get-tuple-element.65), channel_id=1, source_target_pairs={{1,0},{2,1},{3,2},{4,3},{5,4},{6,5},{7,6},{8,7},{9,8},{10,9},{11,1... | collective-permute-start | bytes 98312 | tf_op jit(solution)/shard_map/ppermute | solution.py:378
  51.5 9.6 %collective-permute-start.2 = (f32[4,8,1,256]{3,2,1,0:T(1,128)S(1)}, f32[4,8,1,256]{3,2,1,0:T(1,128)S(1)}, u32[]{:S(2)}, u32[]{:S(2)}) collective-permute-start(f32[4,8,1,256]{3,2,1,0:T(1,128)S(1)} %get-tuple-element.66), channel_id=1, source_target_pairs={{0,1},{1,2},{2,3},{3,4},{4,5},{5,6},{6,7},{7,8},{8,9},{9,10},{10,1... | collective-permute-start | bytes 98312 | tf_op jit(solution)/shard_map/ppermute | solution.py:378
  56.7 4.4 %collective-permute-start.1 = (f32[4,16,256]{2,1,0:T(8,128)S(1)}, f32[4,16,256]{2,1,0:T(8,128)S(1)}, u32[]{:S(2)}, u32[]{:S(2)}) collective-permute-start(f32[4,16,256]{2,1,0:T(8,128)S(1)} %get-tuple-element.67), channel_id=1, source_target_pairs={{16,0},{32,16},{48,32},{64,48},{80,64},{96,80},{112,96},{17,1},{33... | collective-permute-start | bytes 196616 | tf_op jit(solution)/shard_map/ppermute | solution.py:378
  58.6 5.6 %collective-permute-start = (f32[4,16,256]{2,1,0:T(8,128)S(1)}, f32[4,16,256]{2,1,0:T(8,128)S(1)}, u32[]{:S(2)}, u32[]{:S(2)}) collective-permute-start(f32[4,16,256]{2,1,0:T(8,128)S(1)} %get-tuple-element.68), channel_id=1, source_target_pairs={{0,16},{16,32},{32,48},{48,64},{64,80},{80,96},{96,112},{1,17},{17... | collective-permute-start | bytes 196616 | tf_op jit(solution)/shard_map/ppermute | solution.py:378
  66.2 21.2 %all-to-all-start.2 = ((bf16[128,16,128]{2,1,0:T(8,128)(2,1)}), bf16[128,16,128]{2,1,0:T(8,128)(2,1)S(1)}, u32[]{:S(2)}, u32[]{:S(2)}) async-start(bf16[128,16,128]{2,1,0:T(8,128)(2,1)} %bitcast.14), calls=%async_computation.2 | async-start | bytes 1048576 | tf_op jit(solution)/shard_map/all_to_all | solution.py:366
  87.5 2.2 %copy-start.1 = (bf16[128,128,128]{2,1,0:T(8,128)(2,1)S(1)}, bf16[128,128,128]{2,1,0:T(8,128)(2,1)}, u32[]{:S(2)}) copy-start(bf16[128,128,128]{2,1,0:T(8,128)(2,1)} %table_ref.5) | copy-start | bytes 12582916
  95.2 24.3 %all-to-all-start.3 = ((bf16[128,16,128]{2,1,0:T(8,128)(2,1)}), bf16[128,16,128]{2,1,0:T(8,128)(2,1)S(1)}, u32[]{:S(2)}, u32[]{:S(2)}) async-start(bf16[128,16,128]{2,1,0:T(8,128)(2,1)} %bitcast.16), calls=%async_computation.3 | async-start | bytes 1048576 | tf_op jit(solution)/shard_map/all_to_all | solution.py:366
  102.5 17.1 %collective-permute-start.4 = (f32[4,16,256]{2,1,0:T(8,128)S(1)}, f32[4,16,256]{2,1,0:T(8,128)S(1)}, u32[]{:S(2)}, u32[]{:S(2)}) collective-permute-start(f32[4,16,256]{2,1,0:T(8,128)S(1)} %get-tuple-element.44), channel_id=1, source_target_pairs={{0,16},{16,32},{32,48},{48,64},{64,80},{80,96},{96,112},{1,17},{17... | collective-permute-start | bytes 196616 | tf_op jit(solution)/shard_map/ppermute | solution.py:378
  104.5 15.0 %collective-permute-start.5 = (f32[4,16,256]{2,1,0:T(8,128)S(1)}, f32[4,16,256]{2,1,0:T(8,128)S(1)}, u32[]{:S(2)}, u32[]{:S(2)}) collective-permute-start(f32[4,16,256]{2,1,0:T(8,128)S(1)} %get-tuple-element.45), channel_id=1, source_target_pairs={{16,0},{32,16},{48,32},{64,48},{80,64},{96,80},{112,96},{17,1},{33... | collective-permute-start | bytes 196616 | tf_op jit(solution)/shard_map/ppermute | solution.py:378
  108.0 5.9 %collective-permute-start.6 = (f32[4,8,1,256]{3,2,1,0:T(1,128)S(1)}, f32[4,8,1,256]{3,2,1,0:T(1,128)S(1)}, u32[]{:S(2)}, u32[]{:S(2)}) collective-permute-start(f32[4,8,1,256]{3,2,1,0:T(1,128)S(1)} %get-tuple-element.46), channel_id=1, source_target_pairs={{0,1},{1,2},{2,3},{3,4},{4,5},{5,6},{6,7},{7,8},{8,9},{9,10},{10,1... | collective-permute-start | bytes 98312 | tf_op jit(solution)/shard_map/ppermute | solution.py:378
  111.6 7.9 %collective-permute-start.7 = (f32[4,8,1,256]{3,2,1,0:T(1,128)S(1)}, f32[4,8,1,256]{3,2,1,0:T(1,128)S(1)}, u32[]{:S(2)}, u32[]{:S(2)}) collective-permute-start(f32[4,8,1,256]{3,2,1,0:T(1,128)S(1)} %get-tuple-element.47), channel_id=1, source_target_pairs={{1,0},{2,1},{3,2},{4,3},{5,4},{6,5},{7,6},{8,7},{9,8},{10,9},{11,1... | collective-permute-start | bytes 98312 | tf_op jit(solution)/shard_map/ppermute | solution.py:378
  121.6 21.0 %all-to-all-start.4 = ((bf16[128,16,128]{2,1,0:T(8,128)(2,1)}), bf16[128,16,128]{2,1,0:T(8,128)(2,1)S(1)}, u32[]{:S(2)}, u32[]{:S(2)}) async-start(bf16[128,16,128]{2,1,0:T(8,128)(2,1)} %bitcast.18), calls=%async_computation.4 | async-start | bytes 1048576 | tf_op jit(solution)/shard_map/all_to_all | solution.py:366
  142.6 2.2 %copy-start.2 = (bf16[128,128,128]{2,1,0:T(8,128)(2,1)S(1)}, bf16[128,128,128]{2,1,0:T(8,128)(2,1)}, u32[]{:S(2)}) copy-start(bf16[128,128,128]{2,1,0:T(8,128)(2,1)} %table_ref.5) | copy-start | bytes 12582916
  150.3 24.3 %all-to-all-start.5 = ((bf16[128,16,128]{2,1,0:T(8,128)(2,1)}), bf16[128,16,128]{2,1,0:T(8,128)(2,1)S(1)}, u32[]{:S(2)}, u32[]{:S(2)}) async-start(bf16[128,16,128]{2,1,0:T(8,128)(2,1)} %bitcast.20), calls=%async_computation.5 | async-start | bytes 1048576 | tf_op jit(solution)/shard_map/all_to_all | solution.py:366
  157.5 17.1 %collective-permute-start.8 = (f32[4,16,256]{2,1,0:T(8,128)S(1)}, f32[4,16,256]{2,1,0:T(8,128)S(1)}, u32[]{:S(2)}, u32[]{:S(2)}) collective-permute-start(f32[4,16,256]{2,1,0:T(8,128)S(1)} %get-tuple-element.56), channel_id=1, source_target_pairs={{0,16},{16,32},{32,48},{48,64},{64,80},{80,96},{96,112},{1,17},{17... | collective-permute-start | bytes 196616 | tf_op jit(solution)/shard_map/ppermute | solution.py:378
  159.6 15.0 %collective-permute-start.9 = (f32[4,16,256]{2,1,0:T(8,128)S(1)}, f32[4,16,256]{2,1,0:T(8,128)S(1)}, u32[]{:S(2)}, u32[]{:S(2)}) collective-permute-start(f32[4,16,256]{2,1,0:T(8,128)S(1)} %get-tuple-element.57), channel_id=1, source_target_pairs={{16,0},{32,16},{48,32},{64,48},{80,64},{96,80},{112,96},{17,1},{33... | collective-permute-start | bytes 196616 | tf_op jit(solution)/shard_map/ppermute | solution.py:378
  163.1 5.9 %collective-permute-start.10 = (f32[4,8,1,256]{3,2,1,0:T(1,128)S(1)}, f32[4,8,1,256]{3,2,1,0:T(1,128)S(1)}, u32[]{:S(2)}, u32[]{:S(2)}) collective-permute-start(f32[4,8,1,256]{3,2,1,0:T(1,128)S(1)} %get-tuple-element.58), channel_id=1, source_target_pairs={{0,1},{1,2},{2,3},{3,4},{4,5},{5,6},{6,7},{7,8},{8,9},{9,10},{10,1... | collective-permute-start | bytes 98312 | tf_op jit(solution)/shard_map/ppermute | solution.py:378
  166.7 7.9 %collective-permute-start.11 = (f32[4,8,1,256]{3,2,1,0:T(1,128)S(1)}, f32[4,8,1,256]{3,2,1,0:T(1,128)S(1)}, u32[]{:S(2)}, u32[]{:S(2)}) collective-permute-start(f32[4,8,1,256]{3,2,1,0:T(1,128)S(1)} %get-tuple-element.59), channel_id=1, source_target_pairs={{1,0},{2,1},{3,2},{4,3},{5,4},{6,5},{7,6},{8,7},{9,8},{10,9},{11,1... | collective-permute-start | bytes 98312 | tf_op jit(solution)/shard_map/ppermute | solution.py:378
where the time goes:
time: 178 us; the launch traced here: 177 us
  starting transfers between devices  88.5 us (50%)
  Pallas kernels  51.1 us (29%)
  waiting for transfers between devices  19.4 us (11%)
  local copies, waits for them, and re-layouts  14.1 us (8%)
  other arithmetic  2.87 us (2%)
    all_to_all x6, starting transfers between devices, exchange(): lax.all_to_all(payload.reshape(128, 16, 128), AXES, split_axis=0, concat_...  53.4 us
    ppermute x12, starting transfers between devices, shift(): return (lax.ppermute(high, axis, up), lax.ppermute(low, axis, down))  35.1 us
    pallas_call x3, Pallas kernels, body(): elastic, shared = elastic_call(displace, index, fiber, deriv, derivt)  27.6 us
    pallas_call x3, Pallas kernels, body(): couple_call(windex, received, velocity, pick, pickt, weight_table, shared)  16.5 us
    ppermute x12, waiting for transfers between devices, shift(): return (lax.ppermute(high, axis, up), lax.ppermute(low, axis, down))  14.3 us
    unnamed x18, local copies, waits for them, and re-layouts  9.19 us
    pallas_call x3, Pallas kernels, body(): update_call(last)  5.7 us
    all_to_all x6, waiting for transfers between devices, exchange(): lax.all_to_all(payload.reshape(128, 16, 128), AXES, split_axis=0, concat_...  5.03 us
  transfers between devices with their start and end apart: 18, of which 5 were waited for; matrix products, arithmetic and copies ran while one was open for 3% of the time, Pallas kernels for 16%

commit v1 on v0

v1 whole, which is shorter than its diff:
```python
import math

import jax
import jax.numpy as jnp
from jax import lax
from jax.experimental import pallas as pl
from jax.experimental.pallas import tpu as pltpu
from jax.sharding import PartitionSpec as P

STEPS = 3

time_step = 0.1
viscosity = 1.0
sound_square = 1.0
penalty = 4.0
node_mass = 0.5
shear_modulus = 2.0
bulk_modulus = 4.0
fiber_stiff = 2.0
fiber_exponent = 1.0

BF16 = jnp.bfloat16
F32 = jnp.float32
AXES = ("gx", "gy")
FETCH = 7
DEPOSIT = 7
GROUP = 2


def lagrange(degree, position):
    outer = 0.5 * position * position
    ends = jnp.where(degree == 0, outer - 0.5 * position, outer + 0.5 * position)
    return jnp.where(degree == 1, 1.0 - position * position, ends)


def slope(degree, position):
    ends = jnp.where(degree == 0, position - 0.5, position + 0.5)
    return jnp.where(degree == 1, -2.0 * position, ends)


def derivative_matrix(dims, row_axis):
    row = lax.broadcasted_iota(jnp.int32, dims, row_axis)
    column = lax.broadcasted_iota(jnp.int32, dims, 1 - row_axis)
    i = (row * 171) >> 12
    j = (row - 24 * i) >> 3
    point = row & 7
    node = column >> 2
    first = (node * 57) >> 9
    middle = (node * 43) >> 7
    orders = (first, middle - 3 * first, node - 3 * middle)
    coords = (point >> 2, (point >> 1) & 1, point & 1)
    value = jnp.where(((column & 3) == i) & (node < 27), 2.0, 0.0)
    for axis in range(3):
        position = jnp.where(coords[axis] == 0, -1.0 / math.sqrt(3.0), 1.0 / math.sqrt(3.0))
        value = value * jnp.where(
            j == axis, slope(orders[axis], position), lagrange(orders[axis], position)
        )
    return value


def dot(a, b, precision=None):
    return lax.dot_general(
        a, b, (((1,), (0,)), ((), ())), precision=precision, preferred_element_type=F32
    )


def dot_nt(a, b):
    return lax.dot_general(a, b, (((1,), (1,)), ((), ())), preferred_element_type=F32)


def node_onehot(row):
    lane = row & 127
    return jnp.where(lax.broadcasted_iota(jnp.int32, (128, 512), 0) == lane, 1.0, 0.0).astype(BF16)


def node_high(row):
    return jnp.broadcast_to(row >> 7, (8, 512)) - (
        lax.broadcasted_iota(jnp.int32, (8, 512), 0) >> 2
    )


def pick_rows(table, high):
    picked = jnp.where(high == 0, table[0:8], 0.0)
    for r in range(1, 16):
        picked = picked + jnp.where(high == 2 * r, table[8 * r : 8 * r + 8], 0.0)
    return picked + pltpu.roll(picked, 4, 0)


def spread_rows(value, high):
    return jnp.concatenate([jnp.where(high == 2 * r, value, 0.0) for r in range(16)], axis=0)


def both_halves(value, odd):
    turned = pltpu.roll(value, 4, 0)
    low = lax.broadcasted_iota(jnp.int32, value.shape, 0) < 4
    return jnp.where(low, turned, value) if odd else jnp.where(low, value, turned)


def split(value):
    head = value.astype(BF16)
    return head, (value - head.astype(F32)).astype(BF16)


def elastic_kernel(first):
    def kernel(*refs):
        if first:
            (
                elastic_ref, shared_ref, rows_ref, velrows_ref, deriv_ref, derivt_ref, fiber_ref,
            ) = refs[5:12]
            nodal_ref, work_ref, turn_ref = refs[12:15]
            loaded, sems = refs[15:20], refs[20]
            loads = [pltpu.make_async_copy(refs[n], loaded[n], sems.at[n]) for n in range(5)]
            for load in loads:
                load.start()
            disp_ref, vel_ref, conn_ref, share_ref, angle_ref = loaded
            for load in loads:
                load.wait()
            rows_ref[...] = jnp.zeros((128, 128), F32)
            velrows_ref[...] = jnp.zeros((128, 128), F32)
            for h in range(32):
                rows_ref[4 * h : 4 * h + 3, :] = disp_ref[h]
                velrows_ref[4 * h : 4 * h + 3, :] = vel_ref[h]
            deriv_ref[...] = derivative_matrix((72, 112), 0)
            derivt_ref[...] = -0.125 * derivative_matrix((112, 72), 1)
            angles = angle_ref[...]
            cosine, sine = jnp.cos(angles), jnp.sin(angles)
            fiber_ref[0:1, :] = cosine[0:1] * cosine[1:2]
            fiber_ref[1:2, :] = cosine[0:1] * sine[1:2]
            fiber_ref[2:3, :] = sine[0:1]
        else:
            rows_ref, conn_ref, share_ref, deriv_ref, derivt_ref, fiber_ref = refs[:6]
            elastic_ref, shared_ref, nodal_ref, work_ref, turn_ref = refs[6:]
        elastic_forces(
            rows_ref, conn_ref, deriv_ref, derivt_ref, fiber_ref, elastic_ref, nodal_ref, work_ref
        )
        share_forces(elastic_ref, share_ref, shared_ref, turn_ref)

    return kernel


def elastic_forces(
    disp_ref, conn_ref, deriv_ref, derivt_ref, fiber_ref, elastic_ref, nodal_ref, work_ref
):
    head, tail = split(disp_ref[...])
    both = jnp.concatenate([head, tail], axis=1)

    def connect(node):
        return conn_ref[pl.ds(jnp.minimum(node, 26), 1), :]

    def fetch(turn, carry):
        for pair in [turn * FETCH + u for u in range(FETCH)]:
            halves = []
            for s in range(2):
                row = connect(2 * pair + s)
                hot = node_onehot(row)
                table = dot(both, jnp.concatenate([hot, hot], axis=0))
                halves.append(pick_rows(table, node_high(row)))
            low = lax.broadcasted_iota(jnp.int32, (8, 512), 0) < 4
            nodal_ref[pl.ds(pl.multiple_of(8 * pair, 8), 8), :] = jnp.where(
                low, halves[0], halves[1]
            )
        return carry

    lax.fori_loop(0, 14 // FETCH, fetch, 0)
    work_ref[...] = dot(deriv_ref[...], nodal_ref[...], lax.Precision.HIGHEST)

    def entry(i, j):
        value = work_ref[8 * (3 * i + j) : 8 * (3 * i + j) + 8, :]
        return value + 1.0 if i == j else value

    F = [[entry(i, j) for j in range(3)] for i in range(3)]
    fiber = [fiber_ref[j : j + 1, :] for j in range(3)]

    def cofactor(i, j):
        i1, i2, j1, j2 = (i + 1) % 3, (i + 2) % 3, (j + 1) % 3, (j + 2) % 3
        return F[i1][j1] * F[i2][j2] - F[i1][j2] * F[i2][j1]

    cof = [[cofactor(i, j) for j in range(3)] for i in range(3)]
    volume = F[0][0] * cof[0][0] + F[0][1] * cof[0][1] + F[0][2] * cof[0][2]
    along = [F[i][0] * fiber[0] + F[i][1] * fiber[1] + F[i][2] * fiber[2] for i in range(3)]
    excess = along[0] * along[0] + along[1] * along[1] + along[2] * along[2] - 1.0
    weight = 2.0 * fiber_stiff * excess * jnp.exp(fiber_exponent * excess * excess)
    factor = bulk_modulus * (volume - 1.0) - shear_modulus
    for i in range(3):
        pulled = weight * along[i]
        for j in range(3):
            work_ref[8 * (3 * i + j) : 8 * (3 * i + j) + 8, :] = (
                shear_modulus * F[i][j] + factor * cof[i][j] + pulled * fiber[j]
            )
    nodal_ref[...] = dot(derivt_ref[...], work_ref[...], lax.Precision.HIGHEST)

    def deposit(turn, total):
        for pair in [turn * DEPOSIT + u for u in range(DEPOSIT)]:
            rows = nodal_ref[pl.ds(pl.multiple_of(8 * pair, 8), 8), :]
            for s in range(2):
                row = connect(2 * pair + s)
                high = node_high(row)
                value_head, value_tail = split(both_halves(rows, s == 1))
                left = jnp.concatenate(
                    [
                        spread_rows(value_head.astype(F32), high),
                        spread_rows(value_tail.astype(F32), high),
                    ],
                    axis=0,
                ).astype(BF16)
                both_parts = dot_nt(left, node_onehot(row))
                total = total + both_parts[:128] + both_parts[128:]
        return total

    elastic_ref[...] = lax.fori_loop(0, 14 // DEPOSIT, deposit, jnp.zeros((128, 128), F32))


def share_row(share_ref, t):
    return jnp.concatenate([share_ref[4 * t + u : 4 * t + u + 1, :] for u in range(4)], axis=1)


def share_forces(elastic_ref, share_ref, shared_ref, turn_ref):
    sent = elastic_ref[...].astype(BF16)
    turn_ref[...] = jnp.zeros((128, 128), F32)
    for t in range(4):
        row = share_row(share_ref, t)
        picked = pick_rows(dot(sent, node_onehot(row)), node_high(row))
        for jj in range(4):
            turn_ref[16 * t + 4 * jj : 16 * t + 4 * jj + 4, :] = picked[0:4, 128 * jj : 128 * jj + 128]
    shared_ref[...] = turn_ref[...].T


def take_plane(rows_ref, q, stride):
    pieces = [rows_ref[pl.ds(3 * j + q, 128, stride=stride), :] for j in range(4)]
    return jnp.concatenate(pieces, axis=0).astype(BF16)


def put_plane(rows_ref, q, stride, plane):
    for j in range(4):
        rows_ref[pl.ds(3 * j + q, 128, stride=stride), :] = plane[128 * j : 128 * j + 128]


def couple_kernel(
    windex_ref, recv_ref, vel_ref, pick_ref, pickt_ref, table_ref, shared_ref,
    payload_ref, coupling_ref, rows_ref, chosen_ref, spread_ref, buffer_ref, sems,
):
    for g in range(8):
        for s in range(4):
            for k in range(4):
                pltpu.make_async_copy(
                    table_ref.at[windex_ref[k, 4 * g + s]],
                    buffer_ref.at[16 * g + 4 * s + k],
                    sems.at[g],
                ).start()
    rows_ref[0:1536, :] = recv_ref[...].astype(F32)
    chosen_ref[...] = jnp.zeros((512, 128), F32)
    pick = pick_ref[...]
    for q in range(3):
        chosen_ref[pl.ds(q, 128, stride=4), :] = dot(pick, take_plane(rows_ref, q, 12))

    def group(g, carry):
        part = pl.ds(pl.multiple_of(16 * g, 16), 16)
        pltpu.make_async_copy(table_ref.at[pl.ds(0, 16)], buffer_ref.at[part], sems.at[g]).wait()
        start = pl.multiple_of(16 * g, 16)
        left = jnp.concatenate(
            [chosen_ref[pl.ds(128 * k + start, 16), :] for k in range(4)], axis=1
        ).astype(BF16)
        owner = lax.broadcasted_iota(jnp.int32, (16, 128), 0) >> 2
        weights = []
        sampled = jnp.zeros((16, 128), F32)
        for s in range(4):
            weight = jnp.concatenate(
                [buffer_ref[16 * g + 4 * s + k] for k in range(4)], axis=1
            )
            weights.append(weight)
            sampled = jnp.where(owner == s, dot_nt(left, weight), sampled)
        coupling = penalty * (sampled - vel_ref[pl.ds(start, 16), :])
        coupling_ref[pl.ds(start, 16), :] = coupling
        pushed = (-coupling).astype(BF16)
        wide_owner = lax.broadcasted_iota(jnp.int32, (16, 512), 0) >> 2
        out = jnp.zeros((16, 512), F32)
        for s in range(4):
            out = jnp.where(wide_owner == s, dot(pushed, weights[s]), out)
        for k in range(4):
            spread_ref[pl.ds(128 * k + start, 16), :] = out[:, 128 * k : 128 * k + 128]
        return carry

    def groups(turn, carry):
        for u in range(GROUP):
            group(turn * GROUP + u, carry)
        return carry

    lax.fori_loop(0, 8 // GROUP, groups, 0)
    pickt = pickt_ref[...]
    for q in range(3):
        head, tail = split(spread_ref[pl.ds(q, 128, stride=4), :])
        put_plane(rows_ref, q, 14, dot(pickt, jnp.concatenate([head, tail], axis=0)))
    rows_ref[pl.ds(12, 128, stride=14), :] = shared_ref[...]
    rows_ref[pl.ds(13, 128, stride=14), :] = jnp.zeros((128, 128), F32)
    payload_ref[...] = rows_ref[...].astype(BF16)


def write_payload(send, blocks_ref, rows_ref, payload_ref):
    sent = dot(send, blocks_ref[...])
    for q in range(3):
        put_plane(rows_ref, q, 12, sent[:, 128 * q : 128 * q + 128])
    payload_ref[...] = rows_ref[0:1536, :].astype(BF16)


def store_blocks(blocks_ref, x, q, plane):
    for half in range(2):
        blocks_ref[128 * half + 16 * x : 128 * half + 16 * x + 16, 128 * q : 128 * q + 128] = plane[
            :, 128 * half : 128 * half + 128
        ].astype(BF16)


def pack_kernel(state_ref, send_ref, payload_ref, blocks_ref, rows_ref):
    for q in range(3):
        for x in range(8):
            store_blocks(blocks_ref, x, q, state_ref[q, x])
    write_payload(send_ref[...], blocks_ref, rows_ref, payload_ref)


def update_kernel(last):
    def kernel(
        recv_ref, state_ref, xlow_ref, xhigh_ref, ylow_ref, yhigh_ref, sendt_ref, send_ref,
        elastic_ref, coupling_ref, vel_ref, disp_ref, share_ref, *rest,
    ):
        if last:
            new_ref, velout_ref, dispout_ref, rows_ref, force_ref, turn_ref = rest
        else:
            (
                new_ref, velout_ref, dispout_ref, payload_ref, xlowout_ref, xhighout_ref,
                ylowout_ref, yhighout_ref, rows_ref, force_ref, turn_ref, blocks_ref,
            ) = rest
        rows_ref[...] = recv_ref[...].astype(F32)
        planes = jnp.concatenate(
            [take_plane(rows_ref, q, 14) for q in range(3)], axis=1
        )
        force_ref[...] = dot(sendt_ref[...], planes)

        turn_ref[...] = rows_ref[pl.ds(12, 128, stride=14), :].T
        total = elastic_ref[...]
        for t in range(4):
            row = share_row(share_ref, t)
            pieces = []
            for jj in range(4):
                first = 16 * t + 8 * (jj // 2)
                pieces.append(both_halves(turn_ref[first : first + 8, :], jj % 2 == 1))
            left = spread_rows(jnp.concatenate(pieces, axis=1), node_high(row)).astype(BF16)
            total = total + dot_nt(left, node_onehot(row))
        velocity = vel_ref[...] + time_step / node_mass * (total + coupling_ref[...])
        displace = disp_ref[...] + time_step * velocity
        if last:
            for h in range(32):
                velout_ref[h] = velocity[4 * h : 4 * h + 3]
                dispout_ref[h] = displace[4 * h : 4 * h + 3]
        else:
            velout_ref[...] = velocity
            dispout_ref[...] = displace

        yrow = lax.broadcasted_iota(jnp.int32, (16, 256), 0)
        zlane = lax.broadcasted_iota(jnp.int32, (16, 256), 1)

        def around(f, x):
            centre = state_ref[f, x]
            xm = xlow_ref[f] if x == 0 else state_ref[f, x - 1]
            xp = xhigh_ref[f] if x == 7 else state_ref[f, x + 1]
            ym = jnp.where(yrow == 0, ylow_ref[f, x], pltpu.roll(centre, 1, 0))
            yp = jnp.where(yrow == 15, yhigh_ref[f, x], pltpu.roll(centre, 15, 0))
            zm = jnp.where(zlane == 0, 0.0, pltpu.roll(centre, 1, 1))
            zp = jnp.where(zlane == 255, 0.0, pltpu.roll(centre, 255, 1))
            return centre, ((xm, xp), (ym, yp), (zm, zp))

        for x in range(8):
            density, near = around(3, x)
            divergence = jnp.zeros((16, 256), F32)
            for q in range(3):
                centre, pairs = around(q, x)
                laplace = -6.0 * centre
                for below, above in pairs:
                    laplace = laplace + (below + above)
                gradient = 0.5 * (near[q][1] - near[q][0])
                below, above = pairs[q]
                divergence = divergence + 0.5 * (
                    (1.0 + near[q][1]) * above - (1.0 + near[q][0]) * below
                )
                force = jnp.concatenate(
                    [
                        force_ref[128 * h + 16 * x : 128 * h + 16 * x + 16, 128 * q : 128 * q + 128]
                        for h in range(2)
                    ],
                    axis=1,
                )
                fresh = centre + time_step * (
                    viscosity * laplace - sound_square * gradient + force
                )
                new_ref[q, x] = fresh
                if not last:
                    store_blocks(blocks_ref, x, q, fresh)
                    put_edges(q, x, fresh, xlowout_ref, xhighout_ref, ylowout_ref, yhighout_ref)
            fresh = density - time_step * divergence
            new_ref[3, x] = fresh
            if not last:
                put_edges(3, x, fresh, xlowout_ref, xhighout_ref, ylowout_ref, yhighout_ref)
        if not last:
            write_payload(send_ref[...], blocks_ref, rows_ref, payload_ref)

    return kernel


def put_edges(f, x, fresh, xlowout_ref, xhighout_ref, ylowout_ref, yhighout_ref):
    if x == 0:
        xlowout_ref[f] = fresh
    if x == 7:
        xhighout_ref[f] = fresh
    ylowout_ref[f, x] = fresh[0:1]
    yhighout_ref[f, x] = fresh[15:16]


VMEM = pl.BlockSpec(memory_space=pltpu.VMEM)
SMEM = pl.BlockSpec(memory_space=pltpu.SMEM)
HBM = pl.BlockSpec(memory_space=pltpu.HBM)


def far(array):
    return pltpu.with_memory_space_constraint(array, pltpu.HBM)


def shape(dims, dtype=F32):
    return jax.ShapeDtypeStruct(dims, dtype)


def call(kernel, outs, specs, scratch, flops, name, mebibytes, out_specs=None):
    return pl.pallas_call(
        kernel,
        out_shape=outs,
        in_specs=specs,
        out_specs=out_specs or [VMEM] * len(outs),
        scratch_shapes=scratch,
        cost_estimate=pl.CostEstimate(flops=flops, transcendentals=0, bytes_accessed=2_000_000),
        compiler_params=pltpu.CompilerParams(vmem_limit_bytes=mebibytes * 1024 * 1024),
        name=name,
    )


def elastic_call(first):
    outs = [shape((128, 128))] * 2
    out_specs = [VMEM] * 2
    specs = [VMEM] * 6
    scratch = [
        pltpu.VMEM((112, 512), F32), pltpu.VMEM((72, 512), F32), pltpu.VMEM((128, 128), F32)
    ]
    if first:
        specs = [HBM] * 5
        scratch = scratch + [
            pltpu.VMEM((32, 3, 128), F32),
            pltpu.VMEM((32, 3, 128), F32),
            pltpu.VMEM((27, 512), jnp.int32),
            pltpu.VMEM((16, 128), jnp.int32),
            pltpu.VMEM((2, 512), F32),
            pltpu.SemaphoreType.DMA((5,)),
        ]
        out_specs = out_specs + [VMEM] * 5
        outs = outs + [shape((128, 128))] * 2
        outs = outs + [shape((72, 112)), shape((112, 72)), shape((3, 512))]
    return call(
        elastic_kernel(first),
        outs,
        specs,
        scratch,
        3_000_000_000,
        "elastic_first" if first else "elastic",
        16,
        out_specs,
    )


def couple_call():
    return call(
        couple_kernel,
        [shape((1792, 128), BF16), shape((128, 128))],
        [SMEM] + [VMEM] * 4 + [HBM, VMEM],
        [
            pltpu.VMEM((1792, 128), F32),
            pltpu.VMEM((512, 128), F32),
            pltpu.VMEM((512, 128), F32),
            pltpu.VMEM((128, 128, 128), BF16),
            pltpu.SemaphoreType.DMA((8,)),
        ],
        1_000_000_000,
        "couple",
        24,
    )


def pack_call():
    return call(
        pack_kernel,
        [shape((1536, 128), BF16)],
        [VMEM] * 2,
        [pltpu.VMEM((256, 384), BF16), pltpu.VMEM((1792, 128), F32)],
        200_000_000,
        "pack",
        16,
    )


def update_call(last):
    nodes = shape((32, 3, 128)) if last else shape((128, 128))
    outs = [shape((4, 8, 16, 256)), nodes, nodes]
    scratch = [
        pltpu.VMEM((1792, 128), F32),
        pltpu.VMEM((256, 384), F32),
        pltpu.VMEM((128, 128), F32),
    ]
    if not last:
        outs = outs + [
            shape((1536, 128), BF16),
            shape((4, 16, 256)),
            shape((4, 16, 256)),
            shape((4, 8, 1, 256)),
            shape((4, 8, 1, 256)),
        ]
        scratch = scratch + [pltpu.VMEM((256, 384), BF16)]
    return call(
        update_kernel(last), outs, [VMEM] * 13, scratch, 500_000_000,
        "finish" if last else "update", 16,
    )


def exchange(payload, dims):
    moved = lax.all_to_all(
        payload.reshape((128,) + dims + (128,)), AXES, split_axis=0, concat_axis=0, tiled=True
    )
    return moved.reshape(-1, 128)


def halo(edges):
    xlow, xhigh, ylow, yhigh = edges

    def shift(low, high, axis):
        size = lax.axis_size(axis)
        up = [(i, i + 1) for i in range(size - 1)]
        down = [(b, a) for a, b in up]
        return lax.ppermute(high, axis, up), lax.ppermute(low, axis, down)

    xm, xp = shift(xlow, xhigh, "gx")
    ym, yp = shift(ylow, yhigh, "gy")
    return xm, xp, ym, yp


def body(
    fluid_state, node_disp, node_vel, fiber_angles, connectivity,
    send_blocks, interp_slots, weight_index, share_nodes, weight_table,
):
    share = share_nodes[0].T
    sends = send_blocks[0].T
    sends = jnp.where(sends < 256, (sends & 1) * 128 + (sends >> 1), -1)
    blocks_range = jnp.arange(256, dtype=jnp.int32)
    slots_range = jnp.arange(512, dtype=jnp.int32)
    send = (sends[:, :, None] == blocks_range[None, None, :]).astype(BF16).reshape(512, 256)
    sendt = (blocks_range[:, None] == sends.reshape(512)[None, :]).astype(BF16)
    slots = (interp_slots & 3) * 128 + (interp_slots >> 2)
    pick = (slots[:, :, None] == slots_range[None, None, :]).astype(BF16).reshape(128, 512)
    flat = slots.reshape(128)
    pickt = (slots_range[:, None] == jnp.concatenate([flat, flat])[None, :]).astype(BF16)

    state = fluid_state
    payload = pack_call()(state, send)[0]
    edges = (state[:, 0], state[:, 7], state[:, :, 0:1], state[:, :, 15:16])
    for step in range(STEPS):
        last = step == STEPS - 1
        received = exchange(payload, (3, 4))
        around = halo(edges)
        if step == 0:
            start_disp = node_disp.reshape(3, 32, 128).transpose(1, 0, 2)
            start_vel = node_vel.reshape(3, 32, 128).transpose(1, 0, 2)
            elastic, shared, displace, velocity, *tables = elastic_call(True)(
                *map(far, (start_disp, start_vel, connectivity, share, fiber_angles))
            )
        else:
            elastic, shared = elastic_call(False)(displace, connectivity, share, *tables)
        outbound, coupling = couple_call()(
            far(weight_index), received, velocity, pick, pickt, far(weight_table), shared
        )
        inbound = exchange(outbound, (7, 2))
        results = update_call(last)(
            inbound, state, *around, sendt, send, elastic, coupling, velocity, displace, share
        )
        state, velocity, displace = results[:3]
        if not last:
            payload = results[3]
            edges = results[4:8]
    out = [nodes.transpose(1, 0, 2).reshape(3, 4096) for nodes in (displace, velocity)]
    return (state, out[0], out[1])


def solution(mesh):
    placed = (
        P(None, "gx", "gy", None),
        P(None, AXES),
        P(None, AXES),
        P(None, AXES),
        P(None, AXES),
        P(AXES, None, None),
        P(None, AXES),
        P(None, AXES),
        P(AXES, None, None),
        P(),
    )
    return jax.shard_map(
        body,
        mesh=mesh,
        in_specs=placed,
        out_specs=(P(None, "gx", "gy", None), P(None, AXES), P(None, AXES)),
        check_vma=False,
    )
```

time: 178 us -> 161 us (0.904)
  local copies, waits for them, and re-layouts: 14.1 us -> 2.23 us
  waiting for transfers between devices: 19.4 us -> 30.4 us
  starting transfers between devices: 88.5 us -> 81 us
  Pallas kernels: 51.1 us -> 44 us
    all_to_all x6, waiting for transfers between devices: 5.03 us -> 15.7 us  [exchange(): lax.all_to_all(payload.reshape((128,) + dims + (128,)), AXES, split_axis=...]
    unnamed x18 -> x8, local copies, waits for them, and re-layouts: 9.19 us -> 1.05 us
    all_to_all x6, starting transfers between devices: 53.4 us -> 45.9 us  [exchange(): lax.all_to_all(payload.reshape((128,) + dims + (128,)), AXES, split_axis=...]
    pallas_call x7, Pallas kernels: 45.4 us -> 38.5 us  [the longest x3 19.7 us: body(): couple_call()]
    reshape x3 -> x0, local copies, waits for them, and re-layouts: 2.13 us -> none  [the longest x1 0.77 us: body(): windex = weight_index.reshape(128)]
  transfers between devices with their start and end apart: 18 -> 18, of which waited for: 5 -> 8; matrix products, arithmetic and copies ran while one was open for 3% -> 1% of each run, Pallas kernels for 16% -> 16%
where the time goes in v1:
time: 161 us; the launch traced here: 160 us
  starting transfers between devices  81 us (50%)
  Pallas kernels  44 us (27%)
  waiting for transfers between devices  30.4 us (19%)
  local copies, waits for them, and re-layouts  2.23 us (1%)
  other arithmetic  1.74 us (1%)
    all_to_all x6, starting transfers between devices, exchange(): lax.all_to_all(payload.reshape((128,) + dims + (128,)), AXES, split_axis=...  45.9 us
    ppermute x12, starting transfers between devices, shift(): return (lax.ppermute(high, axis, up), lax.ppermute(low, axis, down))  35.1 us
    pallas_call x3, Pallas kernels, body(): couple_call()  19.7 us
    all_to_all x6, waiting for transfers between devices, exchange(): lax.all_to_all(payload.reshape((128,) + dims + (128,)), AXES, split_axis=...  15.7 us
    ppermute x12, waiting for transfers between devices, shift(): return (lax.ppermute(high, axis, up), lax.ppermute(low, axis, down))  14.7 us
    pallas_call x2, Pallas kernels, body(): elastic_call(False)(displace, connectivity, share, *tables)  11 us
    pallas_call x1, Pallas kernels, body(): elastic_call(True)  6.68 us
    pallas_call x3, Pallas kernels, body(): update_call(last)  5.52 us
  transfers between devices with their start and end apart: 18, of which 8 were waited for; matrix products, arithmetic and copies ran while one was open for 1% of the time, Pallas kernels for 16%

profile of v1, /device:TPU:14, one launch (start us, length us, event | category | flops | bytes accessed | tf_op | source)
XLA Modules:
  0.0 160.3 jit_solution(4265907861523716469)
XLA Ops:
  0.6 1.1 fusion.4
  1.7 2.7 %collective-permute-start.3 = (f32[4,8,1,256]{3,2,1,0:T(1,128)S(1)}, f32[4,8,1,256]{3,2,1,0:T(1,128)S(1)}, u32[]{:S(2)}, u32[]{:S(2)}) collective-permute-start(f32[4,8,1,256]{3,2,1,0:T(1,128)S(1)} %get-tuple-element.75), channel_id=1, source_target_pairs={{1,0},{2,1},{3,2},{4,3},{5,4},{6,5},{7,6},{8,7},{9,8},{10,9},{11,1... | collective-permute-start | bytes 98312 | tf_op jit(solution)/shard_map/ppermute | solution.py:541
  4.5 5.2 %collective-permute-start.2 = (f32[4,8,1,256]{3,2,1,0:T(1,128)S(1)}, f32[4,8,1,256]{3,2,1,0:T(1,128)S(1)}, u32[]{:S(2)}, u32[]{:S(2)}) collective-permute-start(f32[4,8,1,256]{3,2,1,0:T(1,128)S(1)} %get-tuple-element.76), channel_id=1, source_target_pairs={{0,1},{1,2},{2,3},{3,4},{4,5},{5,6},{6,7},{7,8},{8,9},{9,10},{10,1... | collective-permute-start | bytes 98312 | tf_op jit(solution)/shard_map/ppermute | solution.py:541
  9.7 0.7 select_bitcast_fusion
  10.4 0.1 fusion.send_ref
  10.5 0.0 copy-start
  10.5 1.0 copy-done
  11.6 1.1 pack.1
  12.7 9.9 %all-to-all-start = ((bf16[128,3,4,128]{3,2,1,0:T(4,128)(2,1)}), bf16[128,3,4,128]{3,2,1,0:T(4,128)(2,1)S(1)}, u32[]{:S(2)}, u32[]{:S(2)}) async-start(bf16[128,3,4,128]{3,2,1,0:T(4,128)(2,1)} %bitcast.3), calls=%async_computation | async-start | bytes 786432 | tf_op jit(solution)/shard_map/all_to_all | solution.py:528
  22.6 0.7 shift-right-arithmetic_add_fusion
  23.3 0.1 eq.62
  23.4 0.1 fusion.1.pickt_ref
  23.5 0.1 fusion.3.pick_ref
  23.6 6.7 %elastic_first.1 = (f32[128,128]{1,0:T(8,128)S(1)}, f32[128,128]{1,0:T(8,128)S(1)}, f32[128,128]{1,0:T(8,128)S(1)}, f32[128,128]{1,0:T(8,128)S(1)}, f32[72,112]{...) custom-call(f32[32,3,128]{2,1,0:T(4,128)} %bitcast.53, f32[32,3,128]{2,1,0:T(4,128)} %bitcast.54, ...), custom_call_target="tpu_custom_call" | custom-call | flops 3000000000 | bytes 2000000 | tf_op jit(solution)/shard_map/elastic_first/pallas_call | solution.py:574
  30.2 0.0 copy-start.1
  30.3 0.0 copy-start.2
  30.3 2.7 %all-to-all-done = bf16[128,3,4,128]{3,2,1,0:T(4,128)(2,1)S(1)} async-done(((bf16[128,3,4,128]{3,2,1,0:T(4,128)(2,1)}), bf16[128,3,4,128]{3,2,1,0:T(4,128)(2,1)S(1)}, u32[]{:S(2)}, u32[]{:S(2)}) %all-to-all-start) | async-done | bytes 393248 | tf_op jit(solution)/shard_map/all_to_all | solution.py:528
  33.0 6.7 %couple.3 = (bf16[1792,128]{1,0:T(8,128)(2,1)}, f32[128,128]{1,0:T(8,128)S(1)}) custom-call(s32[4,32]{1,0:T(4,128)} %windex_ref.5, bf16[1536,128]{1,0:T(8,128)(2,1)S(1)} %bitcast.44, f32[128,128]{1,0:T(8,128)S(1)} %get-tuple-element.39.vel_ref, bf16[128,512]{1,0:T(8,128)(2,1)S(1)} %fusion.3.pick_ref, bf16[512,256]{1,0:T(8,128)(2,1)S(1)} %fusion.1.pickt_ref, ...), custom_call_target="tpu_custom_call" | custom-call | flops 1000000000 | bytes 2000000 | tf_op jit(solution)/shard_map/couple/pallas_call | solution.py:579
  39.6 7.0 %all-to-all-start.1 = ((bf16[128,7,2,128]{3,2,1,0:T(2,128)(2,1)}), bf16[128,7,2,128]{3,2,1,0:T(2,128)(2,1)S(1)}, u32[]{:S(2)}, u32[]{:S(2)}) async-start(bf16[128,7,2,128]{3,2,1,0:T(2,128)(2,1)} %bitcast.11), calls=%async_computation.1 | async-start | bytes 917504 | tf_op jit(solution)/shard_map/all_to_all | solution.py:528
  46.7 2.2 %collective-permute-start.1 = (f32[4,16,256]{2,1,0:T(8,128)S(1)}, f32[4,16,256]{2,1,0:T(8,128)S(1)}, u32[]{:S(2)}, u32[]{:S(2)}) collective-permute-start(f32[4,16,256]{2,1,0:T(8,128)S(1)} %get-tuple-element.77), channel_id=1, source_target_pairs={{16,0},{32,16},{48,32},{64,48},{80,64},{96,80},{112,96},{17,1},{33... | collective-permute-start | bytes 196616 | tf_op jit(solution)/shard_map/ppermute | solution.py:541
  48.9 2.1 %collective-permute-start = (f32[4,16,256]{2,1,0:T(8,128)S(1)}, f32[4,16,256]{2,1,0:T(8,128)S(1)}, u32[]{:S(2)}, u32[]{:S(2)}) collective-permute-start(f32[4,16,256]{2,1,0:T(8,128)S(1)} %get-tuple-element.78), channel_id=1, source_target_pairs={{0,16},{16,32},{32,48},{48,64},{64,80},{80,96},{96,112},{1,17},{17... | collective-permute-start | bytes 196616 | tf_op jit(solution)/shard_map/ppermute | solution.py:541
  51.0 0.1 fusion.2.sendt_ref
  51.1 0.9 collective-permute-done.1.xhigh_ref
  52.1 2.4 %collective-permute-done.xlow_ref = f32[4,16,256]{2,1,0:T(8,128)S(1)} collective-permute-done((f32[4,16,256]{2,1,0:T(8,128)S(1)}, f32[4,16,256]{2,1,0:T(8,128)S(1)}, u32[]{:S(2)}, u32[]{:S(2)}) %collective-permute-start) | collective-permute-done | bytes 65568 | tf_op jit(solution)/shard_map/ppermute | solution.py:541
  54.5 3.2 %all-to-all-done.1 = bf16[128,7,2,128]{3,2,1,0:T(2,128)(2,1)S(1)} async-done(((bf16[128,7,2,128]{3,2,1,0:T(2,128)(2,1)}), bf16[128,7,2,128]{3,2,1,0:T(2,128)(2,1)S(1)}, u32[]{:S(2)}, u32[]{:S(2)}) %all-to-all-start.1) | async-done | bytes 458784 | tf_op jit(solution)/shard_map/all_to_all | solution.py:528
  57.7 1.9 %update.2 = (f32[4,8,16,256]{3,2,1,0:T(8,128)S(1)}, f32[128,128]{1,0:T(8,128)S(1)}, f32[128,128]{1,0:T(8,128)S(1)}, bf16[1536,128]{1,0:T(8,128)(2,1)}, f32[4,16,...) custom-call(bf16[1792,128]{1,0:T(8,128)(2,1)S(1)} %bitcast.42, ...), custom_call_target="tpu_custom_call" | custom-call | flops 500000000 | bytes 2000000 | tf_op jit(solution)/shard_map/update/pallas_call | solution.py:583
  59.7 6.5 %all-to-all-start.2 = ((bf16[128,3,4,128]{3,2,1,0:T(4,128)(2,1)}), bf16[128,3,4,128]{3,2,1,0:T(4,128)(2,1)S(1)}, u32[]{:S(2)}, u32[]{:S(2)}) async-start(bf16[128,3,4,128]{3,2,1,0:T(4,128)(2,1)} %bitcast.17), calls=%async_computation.2 | async-start | bytes 786432 | tf_op jit(solution)/shard_map/all_to_all | solution.py:528
  66.2 5.5 %elastic.2 = (f32[128,128]{1,0:T(8,128)S(1)}, f32[128,128]{1,0:T(8,128)S(1)}) custom-call(f32[128,128]{1,0:T(8,128)S(1)} %get-tuple-element.47.refs_0_.disp_ref, s32[27,512]{1,0:T(8,128)S(1)} %copy-done.3, s32[16,128]{1,0:T(8,128)S(1)} %bitcast.49, f32[72,112]{1,0:T(8,128)S(1)} %get-tuple-element.48.refs_3_, f32[112,72]{1,0:T(8,128)S(1)} %get-tuple-element.49.refs_4_, ...), custom_call_target="tpu_custom_call" | custom-call | flops 3000000000 | bytes 2000000 | tf_op jit(solution)/shard_map/elastic/pallas_call | solution.py:578
  71.7 4.9 %all-to-all-done.2 = bf16[128,3,4,128]{3,2,1,0:T(4,128)(2,1)S(1)} async-done(((bf16[128,3,4,128]{3,2,1,0:T(4,128)(2,1)}), bf16[128,3,4,128]{3,2,1,0:T(4,128)(2,1)S(1)}, u32[]{:S(2)}, u32[]{:S(2)}) %all-to-all-start.2) | async-done | bytes 393248 | tf_op jit(solution)/shard_map/all_to_all | solution.py:528
  76.6 6.5 %couple.4 = (bf16[1792,128]{1,0:T(8,128)(2,1)}, f32[128,128]{1,0:T(8,128)S(1)}) custom-call(s32[4,32]{1,0:T(4,128)} %windex_ref.5, bf16[1536,128]{1,0:T(8,128)(2,1)S(1)} %bitcast.46, f32[128,128]{1,0:T(8,128)S(1)} %get-tuple-element.46.vel_ref, bf16[128,512]{1,0:T(8,128)(2,1)S(1)} %fusion.3.pick_ref, bf16[512,256]{1,0:T(8,128)(2,1)S(1)} %fusion.1.pickt_ref, ...), custom_call_target="tpu_custom_call" | custom-call | flops 1000000000 | bytes 2000000 | tf_op jit(solution)/shard_map/couple/pallas_call | solution.py:579
  83.1 6.7 %all-to-all-start.3 = ((bf16[128,7,2,128]{3,2,1,0:T(2,128)(2,1)}), bf16[128,7,2,128]{3,2,1,0:T(2,128)(2,1)S(1)}, u32[]{:S(2)}, u32[]{:S(2)}) async-start(bf16[128,7,2,128]{3,2,1,0:T(2,128)(2,1)} %bitcast.20), calls=%async_computation.3 | async-start | bytes 917504 | tf_op jit(solution)/shard_map/all_to_all | solution.py:528
  89.8 2.0 %collective-permute-start.4 = (f32[4,16,256]{2,1,0:T(8,128)S(1)}, f32[4,16,256]{2,1,0:T(8,128)S(1)}, u32[]{:S(2)}, u32[]{:S(2)}) collective-permute-start(f32[4,16,256]{2,1,0:T(8,128)S(1)} %get-tuple-element.54), channel_id=1, source_target_pairs={{0,16},{16,32},{32,48},{48,64},{64,80},{80,96},{96,112},{1,17},{17... | collective-permute-start | bytes 196616 | tf_op jit(solution)/shard_map/ppermute | solution.py:541
  91.9 3.5 %collective-permute-start.5 = (f32[4,16,256]{2,1,0:T(8,128)S(1)}, f32[4,16,256]{2,1,0:T(8,128)S(1)}, u32[]{:S(2)}, u32[]{:S(2)}) collective-permute-start(f32[4,16,256]{2,1,0:T(8,128)S(1)} %get-tuple-element.55), channel_id=1, source_target_pairs={{16,0},{32,16},{48,32},{64,48},{80,64},{96,80},{112,96},{17,1},{33... | collective-permute-start | bytes 196616 | tf_op jit(solution)/shard_map/ppermute | solution.py:541
  95.4 3.6 %collective-permute-start.6 = (f32[4,8,1,256]{3,2,1,0:T(1,128)S(1)}, f32[4,8,1,256]{3,2,1,0:T(1,128)S(1)}, u32[]{:S(2)}, u32[]{:S(2)}) collective-permute-start(f32[4,8,1,256]{3,2,1,0:T(1,128)S(1)} %get-tuple-element.56), channel_id=1, source_target_pairs={{0,1},{1,2},{2,3},{3,4},{4,5},{5,6},{6,7},{7,8},{8,9},{9,10},{10,1... | collective-permute-start | bytes 98312 | tf_op jit(solution)/shard_map/ppermute | solution.py:541
  99.0 2.3 %collective-permute-start.7 = (f32[4,8,1,256]{3,2,1,0:T(1,128)S(1)}, f32[4,8,1,256]{3,2,1,0:T(1,128)S(1)}, u32[]{:S(2)}, u32[]{:S(2)}) collective-permute-start(f32[4,8,1,256]{3,2,1,0:T(1,128)S(1)} %get-tuple-element.57), channel_id=1, source_target_pairs={{1,0},{2,1},{3,2},{4,3},{5,4},{6,5},{7,6},{8,7},{9,8},{10,9},{11,1... | collective-permute-start | bytes 98312 | tf_op jit(solution)/shard_map/ppermute | solution.py:541
  101.3 5.6 %collective-permute-done.7.yhigh_ref = f32[4,8,1,256]{3,2,1,0:T(1,128)S(1)} collective-permute-done((f32[4,8,1,256]{3,2,1,0:T(1,128)S(1)}, f32[4,8,1,256]{3,2,1,0:T(1,128)S(1)}, u32[]{:S(2)}, u32[]{:S(2)}) %collective-permute-start.7) | collective-permute-done | bytes 32800 | tf_op jit(solution)/shard_map/ppermute | solution.py:541
  106.9 1.9 %update.3 = (f32[4,8,16,256]{3,2,1,0:T(8,128)S(1)}, f32[128,128]{1,0:T(8,128)S(1)}, f32[128,128]{1,0:T(8,128)S(1)}, bf16[1536,128]{1,0:T(8,128)(2,1)}, f32[4,16,...) custom-call(bf16[1792,128]{1,0:T(8,128)(2,1)S(1)} %bitcast.41, ...), custom_call_target="tpu_custom_call" | custom-call | flops 500000000 | bytes 2000000 | tf_op jit(solution)/shard_map/update/pallas_call | solution.py:583
  108.9 9.2 %all-to-all-start.4 = ((bf16[128,3,4,128]{3,2,1,0:T(4,128)(2,1)}), bf16[128,3,4,128]{3,2,1,0:T(4,128)(2,1)S(1)}, u32[]{:S(2)}, u32[]{:S(2)}) async-start(bf16[128,3,4,128]{3,2,1,0:T(4,128)(2,1)} %bitcast.22), calls=%async_computation.4 | async-start | bytes 786432 | tf_op jit(solution)/shard_map/all_to_all | solution.py:528
  118.1 5.5 %elastic.3 = (f32[128,128]{1,0:T(8,128)S(1)}, f32[128,128]{1,0:T(8,128)S(1)}) custom-call(f32[128,128]{1,0:T(8,128)S(1)} %get-tuple-element.62.refs_0_.disp_ref, s32[27,512]{1,0:T(8,128)S(1)} %copy-done.3, s32[16,128]{1,0:T(8,128)S(1)} %bitcast.51, f32[72,112]{1,0:T(8,128)S(1)} %get-tuple-element.48.refs_3_, f32[112,72]{1,0:T(8,128)S(1)} %get-tuple-element.49.refs_4_, ...), custom_call_target="tpu_custom_call" | custom-call | flops 3000000000 | bytes 2000000 | tf_op jit(solution)/shard_map/elastic/pallas_call | solution.py:578
  123.6 4.9 %all-to-all-done.4 = bf16[128,3,4,128]{3,2,1,0:T(4,128)(2,1)S(1)} async-done(((bf16[128,3,4,128]{3,2,1,0:T(4,128)(2,1)}), bf16[128,3,4,128]{3,2,1,0:T(4,128)(2,1)S(1)}, u32[]{:S(2)}, u32[]{:S(2)}) %all-to-all-start.4) | async-done | bytes 393248 | tf_op jit(solution)/shard_map/all_to_all | solution.py:528
  128.5 6.5 %couple.5 = (bf16[1792,128]{1,0:T(8,128)(2,1)}, f32[128,128]{1,0:T(8,128)S(1)}) custom-call(s32[4,32]{1,0:T(4,128)} %windex_ref.5, bf16[1536,128]{1,0:T(8,128)(2,1)S(1)} %bitcast.45, f32[128,128]{1,0:T(8,128)S(1)} %get-tuple-element.61.vel_ref, bf16[128,512]{1,0:T(8,128)(2,1)S(1)} %fusion.3.pick_ref, bf16[512,256]{1,0:T(8,128)(2,1)S(1)} %fusion.1.pickt_ref, ...), custom_call_target="tpu_custom_call" | custom-call | flops 1000000000 | bytes 2000000 | tf_op jit(solution)/shard_map/couple/pallas_call | solution.py:579
  135.0 6.5 %all-to-all-start.5 = ((bf16[128,7,2,128]{3,2,1,0:T(2,128)(2,1)}), bf16[128,7,2,128]{3,2,1,0:T(2,128)(2,1)S(1)}, u32[]{:S(2)}, u32[]{:S(2)}) async-start(bf16[128,7,2,128]{3,2,1,0:T(2,128)(2,1)} %bitcast.24), calls=%async_computation.5 | async-start | bytes 917504 | tf_op jit(solution)/shard_map/all_to_all | solution.py:528
  141.5 2.0 %collective-permute-start.8 = (f32[4,16,256]{2,1,0:T(8,128)S(1)}, f32[4,16,256]{2,1,0:T(8,128)S(1)}, u32[]{:S(2)}, u32[]{:S(2)}) collective-permute-start(f32[4,16,256]{2,1,0:T(8,128)S(1)} %get-tuple-element.66), channel_id=1, source_target_pairs={{0,16},{16,32},{32,48},{48,64},{64,80},{80,96},{96,112},{1,17},{17... | collective-permute-start | bytes 196616 | tf_op jit(solution)/shard_map/ppermute | solution.py:541
  143.6 3.5 %collective-permute-start.9 = (f32[4,16,256]{2,1,0:T(8,128)S(1)}, f32[4,16,256]{2,1,0:T(8,128)S(1)}, u32[]{:S(2)}, u32[]{:S(2)}) collective-permute-start(f32[4,16,256]{2,1,0:T(8,128)S(1)} %get-tuple-element.67), channel_id=1, source_target_pairs={{16,0},{32,16},{48,32},{64,48},{80,64},{96,80},{112,96},{17,1},{33... | collective-permute-start | bytes 196616 | tf_op jit(solution)/shard_map/ppermute | solution.py:541
  147.1 3.6 %collective-permute-start.10 = (f32[4,8,1,256]{3,2,1,0:T(1,128)S(1)}, f32[4,8,1,256]{3,2,1,0:T(1,128)S(1)}, u32[]{:S(2)}, u32[]{:S(2)}) collective-permute-start(f32[4,8,1,256]{3,2,1,0:T(1,128)S(1)} %get-tuple-element.68), channel_id=1, source_target_pairs={{0,1},{1,2},{2,3},{3,4},{4,5},{5,6},{6,7},{7,8},{8,9},{9,10},{10,1... | collective-permute-start | bytes 98312 | tf_op jit(solution)/shard_map/ppermute | solution.py:541
  150.7 2.3 %collective-permute-start.11 = (f32[4,8,1,256]{3,2,1,0:T(1,128)S(1)}, f32[4,8,1,256]{3,2,1,0:T(1,128)S(1)}, u32[]{:S(2)}, u32[]{:S(2)}) collective-permute-start(f32[4,8,1,256]{3,2,1,0:T(1,128)S(1)} %get-tuple-element.69), channel_id=1, source_target_pairs={{1,0},{2,1},{3,2},{4,3},{5,4},{6,5},{7,6},{8,7},{9,8},{10,9},{11,1... | collective-permute-start | bytes 98312 | tf_op jit(solution)/shard_map/ppermute | solution.py:541
  153.0 5.6 %collective-permute-done.11.yhigh_ref = f32[4,8,1,256]{3,2,1,0:T(1,128)S(1)} collective-permute-done((f32[4,8,1,256]{3,2,1,0:T(1,128)S(1)}, f32[4,8,1,256]{3,2,1,0:T(1,128)S(1)}, u32[]{:S(2)}, u32[]{:S(2)}) %collective-permute-start.11) | collective-permute-done | bytes 32800 | tf_op jit(solution)/shard_map/ppermute | solution.py:541
  158.6 1.6 %finish.1 = (f32[4,8,16,256]{3,2,1,0:T(8,128)}, f32[32,3,128]{2,1,0:T(4,128)}, f32[32,3,128]{2,1,0:T(4,128)}) custom-call(bf16[1792,128]{1,0:T(8,128)(2,1)S(1)} %bitcast.43, f32[4,8,16,256]{3,2,1,0:T(8,128)S(1)} %get-tuple-element.65.state_ref, f32[4,16,256]{2,1,0:T(8,128)S(1)} %collective-permute-done.8.xlow_ref, ...), custom_call_target="tpu_custom_call" | custom-call | flops 500000000 | bytes 2000000 | tf_op jit(solution)/shard_map/finish/pallas_call | solution.py:583
  (16 shorter events, 0.1 us)
Async XLA Ops:
  1.7 49.4 %collective-permute-start.3 = (f32[4,8,1,256]{3,2,1,0:T(1,128)S(1)}, f32[4,8,1,256]{3,2,1,0:T(1,128)S(1)}, u32[]{:S(2)}, u32[]{:S(2)}) collective-permute-start(f32[4,8,1,256]{3,2,1,0:T(1,128)S(1)} %get-tuple-element.75), channel_id=1, source_target_pairs={{1,0},{2,1},{3,2},{4,3},{5,4},{6,5},{7,6},{8,7},{9,8},{10,9},{11,1... | collective-permute-start | bytes 98312 | tf_op jit(solution)/shard_map/ppermute | solution.py:541
  4.5 46.7 %collective-permute-start.2 = (f32[4,8,1,256]{3,2,1,0:T(1,128)S(1)}, f32[4,8,1,256]{3,2,1,0:T(1,128)S(1)}, u32[]{:S(2)}, u32[]{:S(2)}) collective-permute-start(f32[4,8,1,256]{3,2,1,0:T(1,128)S(1)} %get-tuple-element.76), channel_id=1, source_target_pairs={{0,1},{1,2},{2,3},{3,4},{4,5},{5,6},{6,7},{7,8},{8,9},{9,10},{10,1... | collective-permute-start | bytes 98312 | tf_op jit(solution)/shard_map/ppermute | solution.py:541
  10.5 1.0 copy-start
  12.7 20.3 %all-to-all-start = ((bf16[128,3,4,128]{3,2,1,0:T(4,128)(2,1)}), bf16[128,3,4,128]{3,2,1,0:T(4,128)(2,1)S(1)}, u32[]{:S(2)}, u32[]{:S(2)}) async-start(bf16[128,3,4,128]{3,2,1,0:T(4,128)(2,1)} %bitcast.3), calls=%async_computation | async-start | bytes 786432 | tf_op jit(solution)/shard_map/all_to_all | solution.py:528
  30.2 16.4 %copy-start.1 = (f32[4,8,16,256]{3,2,1,0:T(8,128)S(1)}, f32[4,8,16,256]{3,2,1,0:T(8,128)}, u32[]{:S(2)}) copy-start(f32[4,8,16,256]{3,2,1,0:T(8,128)} %state_ref.3) | copy-start | bytes 1572868
  30.3 27.5 %copy-start.2 = (s32[1,128,16]{1,2,0:T(8,128)S(1)}, s32[1,128,16]{1,2,0:T(8,128)}, u32[]{:S(2)}) copy-start(s32[1,128,16]{1,2,0:T(8,128)} %param.18) | copy-start | bytes 24580
  33.0 33.2 %copy-start.3 = (s32[27,512]{1,0:T(8,128)S(1)}, s32[27,512]{1,0:T(8,128)}, u32[]{:S(2)}) copy-start(s32[27,512]{1,0:T(8,128)} %refs_1_.3) | copy-start | bytes 165892
  39.6 18.1 %all-to-all-start.1 = ((bf16[128,7,2,128]{3,2,1,0:T(2,128)(2,1)}), bf16[128,7,2,128]{3,2,1,0:T(2,128)(2,1)S(1)}, u32[]{:S(2)}, u32[]{:S(2)}) async-start(bf16[128,7,2,128]{3,2,1,0:T(2,128)(2,1)} %bitcast.11), calls=%async_computation.1 | async-start | bytes 917504 | tf_op jit(solution)/shard_map/all_to_all | solution.py:528
  46.7 5.3 %collective-permute-start.1 = (f32[4,16,256]{2,1,0:T(8,128)S(1)}, f32[4,16,256]{2,1,0:T(8,128)S(1)}, u32[]{:S(2)}, u32[]{:S(2)}) collective-permute-start(f32[4,16,256]{2,1,0:T(8,128)S(1)} %get-tuple-element.77), channel_id=1, source_target_pairs={{16,0},{32,16},{48,32},{64,48},{80,64},{96,80},{112,96},{17,1},{33... | collective-permute-start | bytes 196616 | tf_op jit(solution)/shard_map/ppermute | solution.py:541
  48.9 5.6 %collective-permute-start = (f32[4,16,256]{2,1,0:T(8,128)S(1)}, f32[4,16,256]{2,1,0:T(8,128)S(1)}, u32[]{:S(2)}, u32[]{:S(2)}) collective-permute-start(f32[4,16,256]{2,1,0:T(8,128)S(1)} %get-tuple-element.78), channel_id=1, source_target_pairs={{0,16},{16,32},{32,48},{48,64},{64,80},{80,96},{96,112},{1,17},{17... | collective-permute-start | bytes 196616 | tf_op jit(solution)/shard_map/ppermute | solution.py:541
  59.7 16.9 %all-to-all-start.2 = ((bf16[128,3,4,128]{3,2,1,0:T(4,128)(2,1)}), bf16[128,3,4,128]{3,2,1,0:T(4,128)(2,1)S(1)}, u32[]{:S(2)}, u32[]{:S(2)}) async-start(bf16[128,3,4,128]{3,2,1,0:T(4,128)(2,1)} %bitcast.17), calls=%async_computation.2 | async-start | bytes 786432 | tf_op jit(solution)/shard_map/all_to_all | solution.py:528
  83.1 23.8 %all-to-all-start.3 = ((bf16[128,7,2,128]{3,2,1,0:T(2,128)(2,1)}), bf16[128,7,2,128]{3,2,1,0:T(2,128)(2,1)S(1)}, u32[]{:S(2)}, u32[]{:S(2)}) async-start(bf16[128,7,2,128]{3,2,1,0:T(2,128)(2,1)} %bitcast.20), calls=%async_computation.3 | async-start | bytes 917504 | tf_op jit(solution)/shard_map/all_to_all | solution.py:528
  89.8 17.1 %collective-permute-start.4 = (f32[4,16,256]{2,1,0:T(8,128)S(1)}, f32[4,16,256]{2,1,0:T(8,128)S(1)}, u32[]{:S(2)}, u32[]{:S(2)}) collective-permute-start(f32[4,16,256]{2,1,0:T(8,128)S(1)} %get-tuple-element.54), channel_id=1, source_target_pairs={{0,16},{16,32},{32,48},{48,64},{64,80},{80,96},{96,112},{1,17},{17... | collective-permute-start | bytes 196616 | tf_op jit(solution)/shard_map/ppermute | solution.py:541
  91.9 15.1 %collective-permute-start.5 = (f32[4,16,256]{2,1,0:T(8,128)S(1)}, f32[4,16,256]{2,1,0:T(8,128)S(1)}, u32[]{:S(2)}, u32[]{:S(2)}) collective-permute-start(f32[4,16,256]{2,1,0:T(8,128)S(1)} %get-tuple-element.55), channel_id=1, source_target_pairs={{16,0},{32,16},{48,32},{64,48},{80,64},{96,80},{112,96},{17,1},{33... | collective-permute-start | bytes 196616 | tf_op jit(solution)/shard_map/ppermute | solution.py:541
  95.4 5.9 %collective-permute-start.6 = (f32[4,8,1,256]{3,2,1,0:T(1,128)S(1)}, f32[4,8,1,256]{3,2,1,0:T(1,128)S(1)}, u32[]{:S(2)}, u32[]{:S(2)}) collective-permute-start(f32[4,8,1,256]{3,2,1,0:T(1,128)S(1)} %get-tuple-element.56), channel_id=1, source_target_pairs={{0,1},{1,2},{2,3},{3,4},{4,5},{5,6},{6,7},{7,8},{8,9},{9,10},{10,1... | collective-permute-start | bytes 98312 | tf_op jit(solution)/shard_map/ppermute | solution.py:541
  99.0 7.9 %collective-permute-start.7 = (f32[4,8,1,256]{3,2,1,0:T(1,128)S(1)}, f32[4,8,1,256]{3,2,1,0:T(1,128)S(1)}, u32[]{:S(2)}, u32[]{:S(2)}) collective-permute-start(f32[4,8,1,256]{3,2,1,0:T(1,128)S(1)} %get-tuple-element.57), channel_id=1, source_target_pairs={{1,0},{2,1},{3,2},{4,3},{5,4},{6,5},{7,6},{8,7},{9,8},{10,9},{11,1... | collective-permute-start | bytes 98312 | tf_op jit(solution)/shard_map/ppermute | solution.py:541
  108.9 19.6 %all-to-all-start.4 = ((bf16[128,3,4,128]{3,2,1,0:T(4,128)(2,1)}), bf16[128,3,4,128]{3,2,1,0:T(4,128)(2,1)S(1)}, u32[]{:S(2)}, u32[]{:S(2)}) async-start(bf16[128,3,4,128]{3,2,1,0:T(4,128)(2,1)} %bitcast.22), calls=%async_computation.4 | async-start | bytes 786432 | tf_op jit(solution)/shard_map/all_to_all | solution.py:528
  135.0 23.6 %all-to-all-start.5 = ((bf16[128,7,2,128]{3,2,1,0:T(2,128)(2,1)}), bf16[128,7,2,128]{3,2,1,0:T(2,128)(2,1)S(1)}, u32[]{:S(2)}, u32[]{:S(2)}) async-start(bf16[128,7,2,128]{3,2,1,0:T(2,128)(2,1)} %bitcast.24), calls=%async_computation.5 | async-start | bytes 917504 | tf_op jit(solution)/shard_map/all_to_all | solution.py:528
  141.5 17.1 %collective-permute-start.8 = (f32[4,16,256]{2,1,0:T(8,128)S(1)}, f32[4,16,256]{2,1,0:T(8,128)S(1)}, u32[]{:S(2)}, u32[]{:S(2)}) collective-permute-start(f32[4,16,256]{2,1,0:T(8,128)S(1)} %get-tuple-element.66), channel_id=1, source_target_pairs={{0,16},{16,32},{32,48},{48,64},{64,80},{80,96},{96,112},{1,17},{17... | collective-permute-start | bytes 196616 | tf_op jit(solution)/shard_map/ppermute | solution.py:541
  143.6 15.1 %collective-permute-start.9 = (f32[4,16,256]{2,1,0:T(8,128)S(1)}, f32[4,16,256]{2,1,0:T(8,128)S(1)}, u32[]{:S(2)}, u32[]{:S(2)}) collective-permute-start(f32[4,16,256]{2,1,0:T(8,128)S(1)} %get-tuple-element.67), channel_id=1, source_target_pairs={{16,0},{32,16},{48,32},{64,48},{80,64},{96,80},{112,96},{17,1},{33... | collective-permute-start | bytes 196616 | tf_op jit(solution)/shard_map/ppermute | solution.py:541
  147.1 5.9 %collective-permute-start.10 = (f32[4,8,1,256]{3,2,1,0:T(1,128)S(1)}, f32[4,8,1,256]{3,2,1,0:T(1,128)S(1)}, u32[]{:S(2)}, u32[]{:S(2)}) collective-permute-start(f32[4,8,1,256]{3,2,1,0:T(1,128)S(1)} %get-tuple-element.68), channel_id=1, source_target_pairs={{0,1},{1,2},{2,3},{3,4},{4,5},{5,6},{6,7},{7,8},{8,9},{9,10},{10,1... | collective-permute-start | bytes 98312 | tf_op jit(solution)/shard_map/ppermute | solution.py:541
  150.7 7.9 %collective-permute-start.11 = (f32[4,8,1,256]{3,2,1,0:T(1,128)S(1)}, f32[4,8,1,256]{3,2,1,0:T(1,128)S(1)}, u32[]{:S(2)}, u32[]{:S(2)}) collective-permute-start(f32[4,8,1,256]{3,2,1,0:T(1,128)S(1)} %get-tuple-element.69), channel_id=1, source_target_pairs={{1,0},{2,1},{3,2},{4,3},{5,4},{6,5},{7,6},{8,7},{9,8},{10,9},{11,1... | collective-permute-start | bytes 98312 | tf_op jit(solution)/shard_map/ppermute | solution.py:541

commit v2 on v1

--- a/solution.py
+++ b/solution.py
@@ -6,6 +6,7 @@
 from jax.experimental import pallas as pl
 from jax.experimental.pallas import tpu as pltpu
 from jax.sharding import PartitionSpec as P
+
 
 STEPS = 3
 
@@ -24,7 +25,7 @@
 AXES = ("gx", "gy")
 FETCH = 7
 DEPOSIT = 7
-GROUP = 2
+GROUP = 8
 
 
 def lagrange(degree, position):
@@ -68,26 +69,36 @@
     return lax.dot_general(a, b, (((1,), (1,)), ((), ())), preferred_element_type=F32)
 
 
+def packed_offset(values, shift):
+    rows = lax.broadcasted_iota(jnp.int32, (16, 512), 0) >> shift
+    return (jnp.broadcast_to(values, (16, 512)) - rows).astype(F32).astype(BF16)
+
+
 def node_onehot(row):
-    lane = row & 127
-    return jnp.where(lax.broadcasted_iota(jnp.int32, (128, 512), 0) == lane, 1.0, 0.0).astype(BF16)
-
-
-def node_high(row):
-    return jnp.broadcast_to(row >> 7, (8, 512)) - (
+    offset = packed_offset(row & 127, 0)
+    one, zero = jnp.ones((16, 512), BF16), jnp.zeros((16, 512), BF16)
+    return jnp.concatenate(
+        [jnp.where(offset == jnp.asarray(16 * r, BF16), one, zero) for r in range(8)], axis=0
+    )
+
+
+def pick_rows(table, row):
+    high = jnp.broadcast_to(row >> 7, (8, 512)) - (
         lax.broadcasted_iota(jnp.int32, (8, 512), 0) >> 2
     )
-
-
-def pick_rows(table, high):
     picked = jnp.where(high == 0, table[0:8], 0.0)
     for r in range(1, 16):
-        picked = picked + jnp.where(high == 2 * r, table[8 * r : 8 * r + 8], 0.0)
+        picked = jnp.where(high == 2 * r, table[8 * r : 8 * r + 8], picked)
     return picked + pltpu.roll(picked, 4, 0)
 
 
-def spread_rows(value, high):
-    return jnp.concatenate([jnp.where(high == 2 * r, value, 0.0) for r in range(16)], axis=0)
+def spread_rows(value, row):
+    high = packed_offset(row >> 7, 2)
+    wide = jnp.concatenate([value, value], axis=0).astype(BF16)
+    zero = jnp.zeros((16, 512), BF16)
+    return jnp.concatenate(
+        [jnp.where(high == jnp.asarray(4 * r, BF16), wide, zero) for r in range(8)], axis=0
+    )
 
 
 def both_halves(value, odd):
@@ -154,7 +165,7 @@
                 row = connect(2 * pair + s)
                 hot = node_onehot(row)
                 table = dot(both, jnp.concatenate([hot, hot], axis=0))
-                halves.append(pick_rows(table, node_high(row)))
+                halves.append(pick_rows(table, row))
             low = lax.broadcasted_iota(jnp.int32, (8, 512), 0) < 4
             nodal_ref[pl.ds(pl.multiple_of(8 * pair, 8), 8), :] = jnp.where(
                 low, halves[0], halves[1]
@@ -194,15 +205,9 @@
             rows = nodal_ref[pl.ds(pl.multiple_of(8 * pair, 8), 8), :]
             for s in range(2):
                 row = connect(2 * pair + s)
-                high = node_high(row)
-                value_head, value_tail = split(both_halves(rows, s == 1))
-                left = jnp.concatenate(
-                    [
-                        spread_rows(value_head.astype(F32), high),
-                        spread_rows(value_tail.astype(F32), high),
-                    ],
-                    axis=0,
-                ).astype(BF16)
+                value = both_halves(rows, s == 1)
+                tail = value - value.astype(BF16).astype(F32)
+                left = jnp.concatenate([spread_rows(value, row), spread_rows(tail, row)], axis=0)
                 both_parts = dot_nt(left, node_onehot(row))
                 total = total + both_parts[:128] + both_parts[128:]
         return total
@@ -219,7 +224,7 @@
     turn_ref[...] = jnp.zeros((128, 128), F32)
     for t in range(4):
         row = share_row(share_ref, t)
-        picked = pick_rows(dot(sent, node_onehot(row)), node_high(row))
+        picked = pick_rows(dot(sent, node_onehot(row)), row)
         for jj in range(4):
             turn_ref[16 * t + 4 * jj : 16 * t + 4 * jj + 4, :] = picked[0:4, 128 * jj : 128 * jj + 128]
     shared_ref[...] = turn_ref[...].T
@@ -342,7 +347,7 @@
             for jj in range(4):
                 first = 16 * t + 8 * (jj // 2)
                 pieces.append(both_halves(turn_ref[first : first + 8, :], jj % 2 == 1))
-            left = spread_rows(jnp.concatenate(pieces, axis=1), node_high(row)).astype(BF16)
+            left = spread_rows(jnp.concatenate(pieces, axis=1), row)
             total = total + dot_nt(left, node_onehot(row))
         velocity = vel_ref[...] + time_step / node_mass * (total + coupling_ref[...])
         displace = disp_ref[...] + time_step * velocity
@@ -426,7 +431,7 @@
     return jax.ShapeDtypeStruct(dims, dtype)
 
 
-def call(kernel, outs, specs, scratch, flops, name, mebibytes, out_specs=None):
+def call(kernel, outs, specs, scratch, flops, mebibytes, out_specs=None):
     return pl.pallas_call(
         kernel,
         out_shape=outs,
@@ -435,7 +440,6 @@
         scratch_shapes=scratch,
         cost_estimate=pl.CostEstimate(flops=flops, transcendentals=0, bytes_accessed=2_000_000),
         compiler_params=pltpu.CompilerParams(vmem_limit_bytes=mebibytes * 1024 * 1024),
-        name=name,
     )
 
 
@@ -459,16 +463,7 @@
         out_specs = out_specs + [VMEM] * 5
         outs = outs + [shape((128, 128))] * 2
         outs = outs + [shape((72, 112)), shape((112, 72)), shape((3, 512))]
-    return call(
-        elastic_kernel(first),
-        outs,
-        specs,
-        scratch,
-        3_000_000_000,
-        "elastic_first" if first else "elastic",
-        16,
-        out_specs,
-    )
+    return call(elastic_kernel(first), outs, specs, scratch, 3_000_000_000, 16, out_specs)
 
 
 def couple_call():
@@ -484,7 +479,6 @@
             pltpu.SemaphoreType.DMA((8,)),
         ],
         1_000_000_000,
-        "couple",
         24,
     )
 
@@ -496,7 +490,6 @@
         [VMEM] * 2,
         [pltpu.VMEM((256, 384), BF16), pltpu.VMEM((1792, 128), F32)],
         200_000_000,
-        "pack",
         16,
     )
 
@@ -520,7 +513,7 @@
         scratch = scratch + [pltpu.VMEM((256, 384), BF16)]
     return call(
         update_kernel(last), outs, [VMEM] * 13, scratch, 500_000_000,
-        "finish" if last else "update", 16,
+        16,
     )
 
 
@@ -564,13 +557,13 @@
     state = fluid_state
     payload = pack_call()(state, send)[0]
     edges = (state[:, 0], state[:, 7], state[:, :, 0:1], state[:, :, 15:16])
+    start_disp = node_disp.reshape(3, 32, 128).transpose(1, 0, 2)
+    start_vel = node_vel.reshape(3, 32, 128).transpose(1, 0, 2)
     for step in range(STEPS):
         last = step == STEPS - 1
         received = exchange(payload, (3, 4))
         around = halo(edges)
         if step == 0:
-            start_disp = node_disp.reshape(3, 32, 128).transpose(1, 0, 2)
-            start_vel = node_vel.reshape(3, 32, 128).transpose(1, 0, 2)
             elastic, shared, displace, velocity, *tables = elastic_call(True)(
                 *map(far, (start_disp, start_vel, connectivity, share, fiber_angles))
             )

time: 161 us -> 160 us (level)
  Pallas kernels: 44 us -> 40.8 us
  waiting for transfers between devices: 30.4 us -> 32.9 us
    all_to_all x6, waiting for transfers between devices: 15.7 us -> 18.3 us  [exchange(): lax.all_to_all(payload.reshape((128,) + dims + (128,)), AXES, split_axis=...]
    pallas_call x2, Pallas kernels: 11 us -> 9.22 us  [body(): elastic_call(False)(displace, connectivity, share, *tables)]
  transfers between devices with their start and end apart: 18 -> 18, of which waited for: 8 -> 8; matrix products, arithmetic and copies ran while one was open for 1% -> 1% of each run, Pallas kernels for 16% -> 14%
where the time goes in v2:
time: 160 us; the launch traced here: 159 us
  starting transfers between devices  80.3 us (50%)
  Pallas kernels  40.8 us (25%)
  waiting for transfers between devices  32.9 us (21%)
  local copies, waits for them, and re-layouts  2.23 us (1%)
  other arithmetic  1.74 us (1%)
    all_to_all x6, starting transfers between devices, exchange(): lax.all_to_all(payload.reshape((128,) + dims + (128,)), AXES, split_axis=...  45.2 us
    ppermute x12, starting transfers between devices, shift(): return (lax.ppermute(high, axis, up), lax.ppermute(low, axis, down))  35.1 us
    pallas_call x3, Pallas kernels, body(): couple_call()  19.4 us
    all_to_all x6, waiting for transfers between devices, exchange(): lax.all_to_all(payload.reshape((128,) + dims + (128,)), AXES, split_axis=...  18.3 us
    ppermute x12, waiting for transfers between devices, shift(): return (lax.ppermute(high, axis, up), lax.ppermute(low, axis, down))  14.6 us
    pallas_call x2, Pallas kernels, body(): elastic_call(False)(displace, connectivity, share, *tables)  9.22 us
    pallas_call x1, Pallas kernels, body(): elastic_call(True)  5.82 us
    pallas_call x3, Pallas kernels, body(): update_call(last)  5.3 us
  transfers between devices with their start and end apart: 18, of which 8 were waited for; matrix products, arithmetic and copies ran while one was open for 1% of the time, Pallas kernels for 14%

profile of v2, /device:TPU:14, one launch (start us, length us, event | category | flops | bytes accessed | tf_op | source)
XLA Modules:
  0.0 159.0 jit_solution(14354720284107259009)
XLA Ops:
  0.6 1.1 fusion.4
  1.7 2.7 %collective-permute-start.3 = (f32[4,8,1,256]{3,2,1,0:T(1,128)S(1)}, f32[4,8,1,256]{3,2,1,0:T(1,128)S(1)}, u32[]{:S(2)}, u32[]{:S(2)}) collective-permute-start(f32[4,8,1,256]{3,2,1,0:T(1,128)S(1)} %get-tuple-element.75), channel_id=1, source_target_pairs={{1,0},{2,1},{3,2},{4,3},{5,4},{6,5},{7,6},{8,7},{9,8},{10,9},{11,1... | collective-permute-start | bytes 98312 | tf_op jit(solution)/shard_map/ppermute | solution.py:534
  4.5 5.2 %collective-permute-start.2 = (f32[4,8,1,256]{3,2,1,0:T(1,128)S(1)}, f32[4,8,1,256]{3,2,1,0:T(1,128)S(1)}, u32[]{:S(2)}, u32[]{:S(2)}) collective-permute-start(f32[4,8,1,256]{3,2,1,0:T(1,128)S(1)} %get-tuple-element.76), channel_id=1, source_target_pairs={{0,1},{1,2},{2,3},{3,4},{4,5},{5,6},{6,7},{7,8},{8,9},{9,10},{10,1... | collective-permute-start | bytes 98312 | tf_op jit(solution)/shard_map/ppermute | solution.py:534
  9.7 0.7 select_bitcast_fusion
  10.4 0.1 fusion.send_ref
  10.5 0.0 copy-start
  10.5 1.0 copy-done
  11.6 1.1 shard_map.121
  12.7 9.9 %all-to-all-start = ((bf16[128,3,4,128]{3,2,1,0:T(4,128)(2,1)}), bf16[128,3,4,128]{3,2,1,0:T(4,128)(2,1)S(1)}, u32[]{:S(2)}, u32[]{:S(2)}) async-start(bf16[128,3,4,128]{3,2,1,0:T(4,128)(2,1)} %bitcast.3), calls=%async_computation | async-start | bytes 786432 | tf_op jit(solution)/shard_map/all_to_all | solution.py:521
  22.6 0.7 shift-right-arithmetic_add_fusion
  23.3 0.1 eq.62
  23.4 0.1 fusion.1.pickt_ref
  23.5 0.1 fusion.3.pick_ref
  23.6 5.8 %shard_map.122 = (f32[128,128]{1,0:T(8,128)S(1)}, f32[128,128]{1,0:T(8,128)S(1)}, f32[128,128]{1,0:T(8,128)S(1)}, f32[128,128]{1,0:T(8,128)S(1)}, f32[72,112]{1,...) custom-call(f32[32,3,128]{2,1,0:T(4,128)} %bitcast.53, f32[32,3,128]{2,1,0:T(4,128)} %bitcast.54, ...), custom_call_target="tpu_custom_call" | custom-call | flops 3000000000 | bytes 2000000 | tf_op jit(solution)/shard_map/pallas_call | solution.py:567
  29.4 0.0 copy-start.1
  29.4 0.0 copy-start.2
  29.4 3.6 %all-to-all-done = bf16[128,3,4,128]{3,2,1,0:T(4,128)(2,1)S(1)} async-done(((bf16[128,3,4,128]{3,2,1,0:T(4,128)(2,1)}), bf16[128,3,4,128]{3,2,1,0:T(4,128)(2,1)S(1)}, u32[]{:S(2)}, u32[]{:S(2)}) %all-to-all-start) | async-done | bytes 393248 | tf_op jit(solution)/shard_map/all_to_all | solution.py:521
  33.0 6.6 %shard_map.123 = (bf16[1792,128]{1,0:T(8,128)(2,1)}, f32[128,128]{1,0:T(8,128)S(1)}) custom-call(s32[4,32]{1,0:T(4,128)} %windex_ref.5, bf16[1536,128]{1,0:T(8,128)(2,1)S(1)} %bitcast.44, f32[128,128]{1,0:T(8,128)S(1)} %get-tuple-element.39.vel_ref, bf16[128,512]{1,0:T(8,128)(2,1)S(1)} %fusion.3.pick_ref, bf16[512,256]{1,0:T(8,128)(2,1)S(1)} %fusion.1.pickt_ref, ...), custom_call_target="tpu_custom_call" | custom-call | flops 1000000000 | bytes 2000000 | tf_op jit(solution)/shard_map/pallas_call | solution.py:572
  39.5 6.5 %all-to-all-start.1 = ((bf16[128,7,2,128]{3,2,1,0:T(2,128)(2,1)}), bf16[128,7,2,128]{3,2,1,0:T(2,128)(2,1)S(1)}, u32[]{:S(2)}, u32[]{:S(2)}) async-start(bf16[128,7,2,128]{3,2,1,0:T(2,128)(2,1)} %bitcast.11), calls=%async_computation.1 | async-start | bytes 917504 | tf_op jit(solution)/shard_map/all_to_all | solution.py:521
  46.1 2.2 %collective-permute-start.1 = (f32[4,16,256]{2,1,0:T(8,128)S(1)}, f32[4,16,256]{2,1,0:T(8,128)S(1)}, u32[]{:S(2)}, u32[]{:S(2)}) collective-permute-start(f32[4,16,256]{2,1,0:T(8,128)S(1)} %get-tuple-element.77), channel_id=1, source_target_pairs={{16,0},{32,16},{48,32},{64,48},{80,64},{96,80},{112,96},{17,1},{33... | collective-permute-start | bytes 196616 | tf_op jit(solution)/shard_map/ppermute | solution.py:534
  48.3 2.1 %collective-permute-start = (f32[4,16,256]{2,1,0:T(8,128)S(1)}, f32[4,16,256]{2,1,0:T(8,128)S(1)}, u32[]{:S(2)}, u32[]{:S(2)}) collective-permute-start(f32[4,16,256]{2,1,0:T(8,128)S(1)} %get-tuple-element.78), channel_id=1, source_target_pairs={{0,16},{16,32},{32,48},{48,64},{64,80},{80,96},{96,112},{1,17},{17... | collective-permute-start | bytes 196616 | tf_op jit(solution)/shard_map/ppermute | solution.py:534
  50.4 0.1 fusion.2.sendt_ref
  50.5 0.9 collective-permute-done.1.xhigh_ref
  51.4 2.4 %collective-permute-done.xlow_ref = f32[4,16,256]{2,1,0:T(8,128)S(1)} collective-permute-done((f32[4,16,256]{2,1,0:T(8,128)S(1)}, f32[4,16,256]{2,1,0:T(8,128)S(1)}, u32[]{:S(2)}, u32[]{:S(2)}) %collective-permute-start) | collective-permute-done | bytes 65568 | tf_op jit(solution)/shard_map/ppermute | solution.py:534
  53.9 3.3 %all-to-all-done.1 = bf16[128,7,2,128]{3,2,1,0:T(2,128)(2,1)S(1)} async-done(((bf16[128,7,2,128]{3,2,1,0:T(2,128)(2,1)}), bf16[128,7,2,128]{3,2,1,0:T(2,128)(2,1)S(1)}, u32[]{:S(2)}, u32[]{:S(2)}) %all-to-all-start.1) | async-done | bytes 458784 | tf_op jit(solution)/shard_map/all_to_all | solution.py:521
  57.1 1.9 %shard_map.124 = (f32[4,8,16,256]{3,2,1,0:T(8,128)S(1)}, f32[128,128]{1,0:T(8,128)S(1)}, f32[128,128]{1,0:T(8,128)S(1)}, bf16[1536,128]{1,0:T(8,128)(2,1)}, f32[...) custom-call(bf16[1792,128]{1,0:T(8,128)(2,1)S(1)} %bitcast.42, ...), custom_call_target="tpu_custom_call" | custom-call | flops 500000000 | bytes 2000000 | tf_op jit(solution)/shard_map/pallas_call | solution.py:576
  59.0 6.5 %all-to-all-start.2 = ((bf16[128,3,4,128]{3,2,1,0:T(4,128)(2,1)}), bf16[128,3,4,128]{3,2,1,0:T(4,128)(2,1)S(1)}, u32[]{:S(2)}, u32[]{:S(2)}) async-start(bf16[128,3,4,128]{3,2,1,0:T(4,128)(2,1)} %bitcast.17), calls=%async_computation.2 | async-start | bytes 786432 | tf_op jit(solution)/shard_map/all_to_all | solution.py:521
  65.5 4.6 %shard_map.125 = (f32[128,128]{1,0:T(8,128)S(1)}, f32[128,128]{1,0:T(8,128)S(1)}) custom-call(f32[128,128]{1,0:T(8,128)S(1)} %get-tuple-element.47.refs_0_.disp_ref, s32[27,512]{1,0:T(8,128)S(1)} %copy-done.3, s32[16,128]{1,0:T(8,128)S(1)} %bitcast.49, f32[72,112]{1,0:T(8,128)S(1)} %get-tuple-element.48.refs_3_, f32[112,72]{1,0:T(8,128)S(1)} %get-tuple-element.49.refs_4_, ...), custom_call_target="tpu_custom_call" | custom-call | flops 3000000000 | bytes 2000000 | tf_op jit(solution)/shard_map/pallas_call | solution.py:571
  70.1 5.7 %all-to-all-done.2 = bf16[128,3,4,128]{3,2,1,0:T(4,128)(2,1)S(1)} async-done(((bf16[128,3,4,128]{3,2,1,0:T(4,128)(2,1)}), bf16[128,3,4,128]{3,2,1,0:T(4,128)(2,1)S(1)}, u32[]{:S(2)}, u32[]{:S(2)}) %all-to-all-start.2) | async-done | bytes 393248 | tf_op jit(solution)/shard_map/all_to_all | solution.py:521
  75.9 6.4 %shard_map.126 = (bf16[1792,128]{1,0:T(8,128)(2,1)}, f32[128,128]{1,0:T(8,128)S(1)}) custom-call(s32[4,32]{1,0:T(4,128)} %windex_ref.5, bf16[1536,128]{1,0:T(8,128)(2,1)S(1)} %bitcast.46, f32[128,128]{1,0:T(8,128)S(1)} %get-tuple-element.46.vel_ref, bf16[128,512]{1,0:T(8,128)(2,1)S(1)} %fusion.3.pick_ref, bf16[512,256]{1,0:T(8,128)(2,1)S(1)} %fusion.1.pickt_ref, ...), custom_call_target="tpu_custom_call" | custom-call | flops 1000000000 | bytes 2000000 | tf_op jit(solution)/shard_map/pallas_call | solution.py:572
  82.3 6.5 %all-to-all-start.3 = ((bf16[128,7,2,128]{3,2,1,0:T(2,128)(2,1)}), bf16[128,7,2,128]{3,2,1,0:T(2,128)(2,1)S(1)}, u32[]{:S(2)}, u32[]{:S(2)}) async-start(bf16[128,7,2,128]{3,2,1,0:T(2,128)(2,1)} %bitcast.20), calls=%async_computation.3 | async-start | bytes 917504 | tf_op jit(solution)/shard_map/all_to_all | solution.py:521
  88.8 2.0 %collective-permute-start.4 = (f32[4,16,256]{2,1,0:T(8,128)S(1)}, f32[4,16,256]{2,1,0:T(8,128)S(1)}, u32[]{:S(2)}, u32[]{:S(2)}) collective-permute-start(f32[4,16,256]{2,1,0:T(8,128)S(1)} %get-tuple-element.54), channel_id=1, source_target_pairs={{0,16},{16,32},{32,48},{48,64},{64,80},{80,96},{96,112},{1,17},{17... | collective-permute-start | bytes 196616 | tf_op jit(solution)/shard_map/ppermute | solution.py:534
  90.9 3.5 %collective-permute-start.5 = (f32[4,16,256]{2,1,0:T(8,128)S(1)}, f32[4,16,256]{2,1,0:T(8,128)S(1)}, u32[]{:S(2)}, u32[]{:S(2)}) collective-permute-start(f32[4,16,256]{2,1,0:T(8,128)S(1)} %get-tuple-element.55), channel_id=1, source_target_pairs={{16,0},{32,16},{48,32},{64,48},{80,64},{96,80},{112,96},{17,1},{33... | collective-permute-start | bytes 196616 | tf_op jit(solution)/shard_map/ppermute | solution.py:534
  94.4 3.6 %collective-permute-start.6 = (f32[4,8,1,256]{3,2,1,0:T(1,128)S(1)}, f32[4,8,1,256]{3,2,1,0:T(1,128)S(1)}, u32[]{:S(2)}, u32[]{:S(2)}) collective-permute-start(f32[4,8,1,256]{3,2,1,0:T(1,128)S(1)} %get-tuple-element.56), channel_id=1, source_target_pairs={{0,1},{1,2},{2,3},{3,4},{4,5},{5,6},{6,7},{7,8},{8,9},{9,10},{10,1... | collective-permute-start | bytes 98312 | tf_op jit(solution)/shard_map/ppermute | solution.py:534
  98.0 2.3 %collective-permute-start.7 = (f32[4,8,1,256]{3,2,1,0:T(1,128)S(1)}, f32[4,8,1,256]{3,2,1,0:T(1,128)S(1)}, u32[]{:S(2)}, u32[]{:S(2)}) collective-permute-start(f32[4,8,1,256]{3,2,1,0:T(1,128)S(1)} %get-tuple-element.57), channel_id=1, source_target_pairs={{1,0},{2,1},{3,2},{4,3},{5,4},{6,5},{7,6},{8,7},{9,8},{10,9},{11,1... | collective-permute-start | bytes 98312 | tf_op jit(solution)/shard_map/ppermute | solution.py:534
  100.3 5.6 %collective-permute-done.7.yhigh_ref = f32[4,8,1,256]{3,2,1,0:T(1,128)S(1)} collective-permute-done((f32[4,8,1,256]{3,2,1,0:T(1,128)S(1)}, f32[4,8,1,256]{3,2,1,0:T(1,128)S(1)}, u32[]{:S(2)}, u32[]{:S(2)}) %collective-permute-start.7) | collective-permute-done | bytes 32800 | tf_op jit(solution)/shard_map/ppermute | solution.py:534
  105.9 1.9 %shard_map.127 = (f32[4,8,16,256]{3,2,1,0:T(8,128)S(1)}, f32[128,128]{1,0:T(8,128)S(1)}, f32[128,128]{1,0:T(8,128)S(1)}, bf16[1536,128]{1,0:T(8,128)(2,1)}, f32[...) custom-call(bf16[1792,128]{1,0:T(8,128)(2,1)S(1)} %bitcast.41, ...), custom_call_target="tpu_custom_call" | custom-call | flops 500000000 | bytes 2000000 | tf_op jit(solution)/shard_map/pallas_call | solution.py:576
  107.8 9.2 %all-to-all-start.4 = ((bf16[128,3,4,128]{3,2,1,0:T(4,128)(2,1)}), bf16[128,3,4,128]{3,2,1,0:T(4,128)(2,1)S(1)}, u32[]{:S(2)}, u32[]{:S(2)}) async-start(bf16[128,3,4,128]{3,2,1,0:T(4,128)(2,1)} %bitcast.22), calls=%async_computation.4 | async-start | bytes 786432 | tf_op jit(solution)/shard_map/all_to_all | solution.py:521
  117.0 4.6 %shard_map.128 = (f32[128,128]{1,0:T(8,128)S(1)}, f32[128,128]{1,0:T(8,128)S(1)}) custom-call(f32[128,128]{1,0:T(8,128)S(1)} %get-tuple-element.62.refs_0_.disp_ref, s32[27,512]{1,0:T(8,128)S(1)} %copy-done.3, s32[16,128]{1,0:T(8,128)S(1)} %bitcast.51, f32[72,112]{1,0:T(8,128)S(1)} %get-tuple-element.48.refs_3_, f32[112,72]{1,0:T(8,128)S(1)} %get-tuple-element.49.refs_4_, ...), custom_call_target="tpu_custom_call" | custom-call | flops 3000000000 | bytes 2000000 | tf_op jit(solution)/shard_map/pallas_call | solution.py:571
  121.6 5.8 %all-to-all-done.4 = bf16[128,3,4,128]{3,2,1,0:T(4,128)(2,1)S(1)} async-done(((bf16[128,3,4,128]{3,2,1,0:T(4,128)(2,1)}), bf16[128,3,4,128]{3,2,1,0:T(4,128)(2,1)S(1)}, u32[]{:S(2)}, u32[]{:S(2)}) %all-to-all-start.4) | async-done | bytes 393248 | tf_op jit(solution)/shard_map/all_to_all | solution.py:521
  127.4 6.4 %shard_map.129 = (bf16[1792,128]{1,0:T(8,128)(2,1)}, f32[128,128]{1,0:T(8,128)S(1)}) custom-call(s32[4,32]{1,0:T(4,128)} %windex_ref.5, bf16[1536,128]{1,0:T(8,128)(2,1)S(1)} %bitcast.45, f32[128,128]{1,0:T(8,128)S(1)} %get-tuple-element.61.vel_ref, bf16[128,512]{1,0:T(8,128)(2,1)S(1)} %fusion.3.pick_ref, bf16[512,256]{1,0:T(8,128)(2,1)S(1)} %fusion.1.pickt_ref, ...), custom_call_target="tpu_custom_call" | custom-call | flops 1000000000 | bytes 2000000 | tf_op jit(solution)/shard_map/pallas_call | solution.py:572
  133.8 6.5 %all-to-all-start.5 = ((bf16[128,7,2,128]{3,2,1,0:T(2,128)(2,1)}), bf16[128,7,2,128]{3,2,1,0:T(2,128)(2,1)S(1)}, u32[]{:S(2)}, u32[]{:S(2)}) async-start(bf16[128,7,2,128]{3,2,1,0:T(2,128)(2,1)} %bitcast.24), calls=%async_computation.5 | async-start | bytes 917504 | tf_op jit(solution)/shard_map/all_to_all | solution.py:521
  140.3 2.0 %collective-permute-start.8 = (f32[4,16,256]{2,1,0:T(8,128)S(1)}, f32[4,16,256]{2,1,0:T(8,128)S(1)}, u32[]{:S(2)}, u32[]{:S(2)}) collective-permute-start(f32[4,16,256]{2,1,0:T(8,128)S(1)} %get-tuple-element.66), channel_id=1, source_target_pairs={{0,16},{16,32},{32,48},{48,64},{64,80},{80,96},{96,112},{1,17},{17... | collective-permute-start | bytes 196616 | tf_op jit(solution)/shard_map/ppermute | solution.py:534
  142.4 3.5 %collective-permute-start.9 = (f32[4,16,256]{2,1,0:T(8,128)S(1)}, f32[4,16,256]{2,1,0:T(8,128)S(1)}, u32[]{:S(2)}, u32[]{:S(2)}) collective-permute-start(f32[4,16,256]{2,1,0:T(8,128)S(1)} %get-tuple-element.67), channel_id=1, source_target_pairs={{16,0},{32,16},{48,32},{64,48},{80,64},{96,80},{112,96},{17,1},{33... | collective-permute-start | bytes 196616 | tf_op jit(solution)/shard_map/ppermute | solution.py:534
  145.9 3.6 %collective-permute-start.10 = (f32[4,8,1,256]{3,2,1,0:T(1,128)S(1)}, f32[4,8,1,256]{3,2,1,0:T(1,128)S(1)}, u32[]{:S(2)}, u32[]{:S(2)}) collective-permute-start(f32[4,8,1,256]{3,2,1,0:T(1,128)S(1)} %get-tuple-element.68), channel_id=1, source_target_pairs={{0,1},{1,2},{2,3},{3,4},{4,5},{5,6},{6,7},{7,8},{8,9},{9,10},{10,1... | collective-permute-start | bytes 98312 | tf_op jit(solution)/shard_map/ppermute | solution.py:534
  149.5 2.3 %collective-permute-start.11 = (f32[4,8,1,256]{3,2,1,0:T(1,128)S(1)}, f32[4,8,1,256]{3,2,1,0:T(1,128)S(1)}, u32[]{:S(2)}, u32[]{:S(2)}) collective-permute-start(f32[4,8,1,256]{3,2,1,0:T(1,128)S(1)} %get-tuple-element.69), channel_id=1, source_target_pairs={{1,0},{2,1},{3,2},{4,3},{5,4},{6,5},{7,6},{8,7},{9,8},{10,9},{11,1... | collective-permute-start | bytes 98312 | tf_op jit(solution)/shard_map/ppermute | solution.py:534
  151.8 5.6 %collective-permute-done.11.yhigh_ref = f32[4,8,1,256]{3,2,1,0:T(1,128)S(1)} collective-permute-done((f32[4,8,1,256]{3,2,1,0:T(1,128)S(1)}, f32[4,8,1,256]{3,2,1,0:T(1,128)S(1)}, u32[]{:S(2)}, u32[]{:S(2)}) %collective-permute-start.11) | collective-permute-done | bytes 32800 | tf_op jit(solution)/shard_map/ppermute | solution.py:534
  157.4 1.6 shard_map.130
  (16 shorter events, 0.1 us)
Async XLA Ops:
  1.7 48.8 %collective-permute-start.3 = (f32[4,8,1,256]{3,2,1,0:T(1,128)S(1)}, f32[4,8,1,256]{3,2,1,0:T(1,128)S(1)}, u32[]{:S(2)}, u32[]{:S(2)}) collective-permute-start(f32[4,8,1,256]{3,2,1,0:T(1,128)S(1)} %get-tuple-element.75), channel_id=1, source_target_pairs={{1,0},{2,1},{3,2},{4,3},{5,4},{6,5},{7,6},{8,7},{9,8},{10,9},{11,1... | collective-permute-start | bytes 98312 | tf_op jit(solution)/shard_map/ppermute | solution.py:534
  4.5 46.0 %collective-permute-start.2 = (f32[4,8,1,256]{3,2,1,0:T(1,128)S(1)}, f32[4,8,1,256]{3,2,1,0:T(1,128)S(1)}, u32[]{:S(2)}, u32[]{:S(2)}) collective-permute-start(f32[4,8,1,256]{3,2,1,0:T(1,128)S(1)} %get-tuple-element.76), channel_id=1, source_target_pairs={{0,1},{1,2},{2,3},{3,4},{4,5},{5,6},{6,7},{7,8},{8,9},{9,10},{10,1... | collective-permute-start | bytes 98312 | tf_op jit(solution)/shard_map/ppermute | solution.py:534
  10.5 1.0 copy-start
  12.7 20.3 %all-to-all-start = ((bf16[128,3,4,128]{3,2,1,0:T(4,128)(2,1)}), bf16[128,3,4,128]{3,2,1,0:T(4,128)(2,1)S(1)}, u32[]{:S(2)}, u32[]{:S(2)}) async-start(bf16[128,3,4,128]{3,2,1,0:T(4,128)(2,1)} %bitcast.3), calls=%async_computation | async-start | bytes 786432 | tf_op jit(solution)/shard_map/all_to_all | solution.py:521
  29.4 16.7 %copy-start.1 = (f32[4,8,16,256]{3,2,1,0:T(8,128)S(1)}, f32[4,8,16,256]{3,2,1,0:T(8,128)}, u32[]{:S(2)}) copy-start(f32[4,8,16,256]{3,2,1,0:T(8,128)} %state_ref.3) | copy-start | bytes 1572868
  29.4 27.7 %copy-start.2 = (s32[1,128,16]{1,2,0:T(8,128)S(1)}, s32[1,128,16]{1,2,0:T(8,128)}, u32[]{:S(2)}) copy-start(s32[1,128,16]{1,2,0:T(8,128)} %param.18) | copy-start | bytes 24580
  33.0 32.6 %copy-start.3 = (s32[27,512]{1,0:T(8,128)S(1)}, s32[27,512]{1,0:T(8,128)}, u32[]{:S(2)}) copy-start(s32[27,512]{1,0:T(8,128)} %refs_1_.3) | copy-start | bytes 165892
  39.5 17.6 %all-to-all-start.1 = ((bf16[128,7,2,128]{3,2,1,0:T(2,128)(2,1)}), bf16[128,7,2,128]{3,2,1,0:T(2,128)(2,1)S(1)}, u32[]{:S(2)}, u32[]{:S(2)}) async-start(bf16[128,7,2,128]{3,2,1,0:T(2,128)(2,1)} %bitcast.11), calls=%async_computation.1 | async-start | bytes 917504 | tf_op jit(solution)/shard_map/all_to_all | solution.py:521
  46.1 5.3 %collective-permute-start.1 = (f32[4,16,256]{2,1,0:T(8,128)S(1)}, f32[4,16,256]{2,1,0:T(8,128)S(1)}, u32[]{:S(2)}, u32[]{:S(2)}) collective-permute-start(f32[4,16,256]{2,1,0:T(8,128)S(1)} %get-tuple-element.77), channel_id=1, source_target_pairs={{16,0},{32,16},{48,32},{64,48},{80,64},{96,80},{112,96},{17,1},{33... | collective-permute-start | bytes 196616 | tf_op jit(solution)/shard_map/ppermute | solution.py:534
  48.3 5.6 %collective-permute-start = (f32[4,16,256]{2,1,0:T(8,128)S(1)}, f32[4,16,256]{2,1,0:T(8,128)S(1)}, u32[]{:S(2)}, u32[]{:S(2)}) collective-permute-start(f32[4,16,256]{2,1,0:T(8,128)S(1)} %get-tuple-element.78), channel_id=1, source_target_pairs={{0,16},{16,32},{32,48},{48,64},{64,80},{80,96},{96,112},{1,17},{17... | collective-permute-start | bytes 196616 | tf_op jit(solution)/shard_map/ppermute | solution.py:534
  59.0 16.9 %all-to-all-start.2 = ((bf16[128,3,4,128]{3,2,1,0:T(4,128)(2,1)}), bf16[128,3,4,128]{3,2,1,0:T(4,128)(2,1)S(1)}, u32[]{:S(2)}, u32[]{:S(2)}) async-start(bf16[128,3,4,128]{3,2,1,0:T(4,128)(2,1)} %bitcast.17), calls=%async_computation.2 | async-start | bytes 786432 | tf_op jit(solution)/shard_map/all_to_all | solution.py:521
  82.3 23.6 %all-to-all-start.3 = ((bf16[128,7,2,128]{3,2,1,0:T(2,128)(2,1)}), bf16[128,7,2,128]{3,2,1,0:T(2,128)(2,1)S(1)}, u32[]{:S(2)}, u32[]{:S(2)}) async-start(bf16[128,7,2,128]{3,2,1,0:T(2,128)(2,1)} %bitcast.20), calls=%async_computation.3 | async-start | bytes 917504 | tf_op jit(solution)/shard_map/all_to_all | solution.py:521
  88.8 17.1 %collective-permute-start.4 = (f32[4,16,256]{2,1,0:T(8,128)S(1)}, f32[4,16,256]{2,1,0:T(8,128)S(1)}, u32[]{:S(2)}, u32[]{:S(2)}) collective-permute-start(f32[4,16,256]{2,1,0:T(8,128)S(1)} %get-tuple-element.54), channel_id=1, source_target_pairs={{0,16},{16,32},{32,48},{48,64},{64,80},{80,96},{96,112},{1,17},{17... | collective-permute-start | bytes 196616 | tf_op jit(solution)/shard_map/ppermute | solution.py:534
  90.9 15.0 %collective-permute-start.5 = (f32[4,16,256]{2,1,0:T(8,128)S(1)}, f32[4,16,256]{2,1,0:T(8,128)S(1)}, u32[]{:S(2)}, u32[]{:S(2)}) collective-permute-start(f32[4,16,256]{2,1,0:T(8,128)S(1)} %get-tuple-element.55), channel_id=1, source_target_pairs={{16,0},{32,16},{48,32},{64,48},{80,64},{96,80},{112,96},{17,1},{33... | collective-permute-start | bytes 196616 | tf_op jit(solution)/shard_map/ppermute | solution.py:534
  94.4 5.9 %collective-permute-start.6 = (f32[4,8,1,256]{3,2,1,0:T(1,128)S(1)}, f32[4,8,1,256]{3,2,1,0:T(1,128)S(1)}, u32[]{:S(2)}, u32[]{:S(2)}) collective-permute-start(f32[4,8,1,256]{3,2,1,0:T(1,128)S(1)} %get-tuple-element.56), channel_id=1, source_target_pairs={{0,1},{1,2},{2,3},{3,4},{4,5},{5,6},{6,7},{7,8},{8,9},{9,10},{10,1... | collective-permute-start | bytes 98312 | tf_op jit(solution)/shard_map/ppermute | solution.py:534
  98.0 7.9 %collective-permute-start.7 = (f32[4,8,1,256]{3,2,1,0:T(1,128)S(1)}, f32[4,8,1,256]{3,2,1,0:T(1,128)S(1)}, u32[]{:S(2)}, u32[]{:S(2)}) collective-permute-start(f32[4,8,1,256]{3,2,1,0:T(1,128)S(1)} %get-tuple-element.57), channel_id=1, source_target_pairs={{1,0},{2,1},{3,2},{4,3},{5,4},{6,5},{7,6},{8,7},{9,8},{10,9},{11,1... | collective-permute-start | bytes 98312 | tf_op jit(solution)/shard_map/ppermute | solution.py:534
  107.8 19.6 %all-to-all-start.4 = ((bf16[128,3,4,128]{3,2,1,0:T(4,128)(2,1)}), bf16[128,3,4,128]{3,2,1,0:T(4,128)(2,1)S(1)}, u32[]{:S(2)}, u32[]{:S(2)}) async-start(bf16[128,3,4,128]{3,2,1,0:T(4,128)(2,1)} %bitcast.22), calls=%async_computation.4 | async-start | bytes 786432 | tf_op jit(solution)/shard_map/all_to_all | solution.py:521
  133.8 23.6 %all-to-all-start.5 = ((bf16[128,7,2,128]{3,2,1,0:T(2,128)(2,1)}), bf16[128,7,2,128]{3,2,1,0:T(2,128)(2,1)S(1)}, u32[]{:S(2)}, u32[]{:S(2)}) async-start(bf16[128,7,2,128]{3,2,1,0:T(2,128)(2,1)} %bitcast.24), calls=%async_computation.5 | async-start | bytes 917504 | tf_op jit(solution)/shard_map/all_to_all | solution.py:521
  140.3 17.1 %collective-permute-start.8 = (f32[4,16,256]{2,1,0:T(8,128)S(1)}, f32[4,16,256]{2,1,0:T(8,128)S(1)}, u32[]{:S(2)}, u32[]{:S(2)}) collective-permute-start(f32[4,16,256]{2,1,0:T(8,128)S(1)} %get-tuple-element.66), channel_id=1, source_target_pairs={{0,16},{16,32},{32,48},{48,64},{64,80},{80,96},{96,112},{1,17},{17... | collective-permute-start | bytes 196616 | tf_op jit(solution)/shard_map/ppermute | solution.py:534
  142.4 15.0 %collective-permute-start.9 = (f32[4,16,256]{2,1,0:T(8,128)S(1)}, f32[4,16,256]{2,1,0:T(8,128)S(1)}, u32[]{:S(2)}, u32[]{:S(2)}) collective-permute-start(f32[4,16,256]{2,1,0:T(8,128)S(1)} %get-tuple-element.67), channel_id=1, source_target_pairs={{16,0},{32,16},{48,32},{64,48},{80,64},{96,80},{112,96},{17,1},{33... | collective-permute-start | bytes 196616 | tf_op jit(solution)/shard_map/ppermute | solution.py:534
  145.9 5.9 %collective-permute-start.10 = (f32[4,8,1,256]{3,2,1,0:T(1,128)S(1)}, f32[4,8,1,256]{3,2,1,0:T(1,128)S(1)}, u32[]{:S(2)}, u32[]{:S(2)}) collective-permute-start(f32[4,8,1,256]{3,2,1,0:T(1,128)S(1)} %get-tuple-element.68), channel_id=1, source_target_pairs={{0,1},{1,2},{2,3},{3,4},{4,5},{5,6},{6,7},{7,8},{8,9},{9,10},{10,1... | collective-permute-start | bytes 98312 | tf_op jit(solution)/shard_map/ppermute | solution.py:534
  149.5 7.9 %collective-permute-start.11 = (f32[4,8,1,256]{3,2,1,0:T(1,128)S(1)}, f32[4,8,1,256]{3,2,1,0:T(1,128)S(1)}, u32[]{:S(2)}, u32[]{:S(2)}) collective-permute-start(f32[4,8,1,256]{3,2,1,0:T(1,128)S(1)} %get-tuple-element.69), channel_id=1, source_target_pairs={{1,0},{2,1},{3,2},{4,3},{5,4},{6,5},{7,6},{8,7},{9,8},{10,9},{11,1... | collective-permute-start | bytes 98312 | tf_op jit(solution)/shard_map/ppermute | solution.py:534

commit v3 on v2

--- a/solution.py
+++ b/solution.py
@@ -314,10 +314,15 @@
         ].astype(BF16)
 
 
-def pack_kernel(state_ref, send_ref, payload_ref, blocks_ref, rows_ref):
-    for q in range(3):
+def pack_kernel(
+    state_ref, send_ref, payload_ref, xlow_ref, xhigh_ref, ylow_ref, yhigh_ref, blocks_ref, rows_ref
+):
+    for f in range(4):
         for x in range(8):
-            store_blocks(blocks_ref, x, q, state_ref[q, x])
+            plane = state_ref[f, x]
+            if f < 3:
+                store_blocks(blocks_ref, x, f, plane)
+            put_edges(f, x, plane, xlow_ref, xhigh_ref, ylow_ref, yhigh_ref)
     write_payload(send_ref[...], blocks_ref, rows_ref, payload_ref)
 
 
@@ -364,8 +369,8 @@
 
         def around(f, x):
             centre = state_ref[f, x]
-            xm = xlow_ref[f] if x == 0 else state_ref[f, x - 1]
-            xp = xhigh_ref[f] if x == 7 else state_ref[f, x + 1]
+            xm = xlow_ref[f].astype(F32) if x == 0 else state_ref[f, x - 1]
+            xp = xhigh_ref[f].astype(F32) if x == 7 else state_ref[f, x + 1]
             ym = jnp.where(yrow == 0, ylow_ref[f, x], pltpu.roll(centre, 1, 0))
             yp = jnp.where(yrow == 15, yhigh_ref[f, x], pltpu.roll(centre, 15, 0))
             zm = jnp.where(zlane == 0, 0.0, pltpu.roll(centre, 1, 1))
@@ -411,9 +416,9 @@
 
 def put_edges(f, x, fresh, xlowout_ref, xhighout_ref, ylowout_ref, yhighout_ref):
     if x == 0:
-        xlowout_ref[f] = fresh
+        xlowout_ref[f] = fresh.astype(BF16)
     if x == 7:
-        xhighout_ref[f] = fresh
+        xhighout_ref[f] = fresh.astype(BF16)
     ylowout_ref[f, x] = fresh[0:1]
     yhighout_ref[f, x] = fresh[15:16]
 
@@ -429,6 +434,9 @@
 
 def shape(dims, dtype=F32):
     return jax.ShapeDtypeStruct(dims, dtype)
+
+
+EDGES = [shape((4, 16, 256), BF16)] * 2 + [shape((4, 8, 1, 256))] * 2
 
 
 def call(kernel, outs, specs, scratch, flops, mebibytes, out_specs=None):
@@ -486,7 +494,7 @@
 def pack_call():
     return call(
         pack_kernel,
-        [shape((1536, 128), BF16)],
+        [shape((1536, 128), BF16)] + EDGES,
         [VMEM] * 2,
         [pltpu.VMEM((256, 384), BF16), pltpu.VMEM((1792, 128), F32)],
         200_000_000,
@@ -503,13 +511,7 @@
         pltpu.VMEM((128, 128), F32),
     ]
     if not last:
-        outs = outs + [
-            shape((1536, 128), BF16),
-            shape((4, 16, 256)),
-            shape((4, 16, 256)),
-            shape((4, 8, 1, 256)),
-            shape((4, 8, 1, 256)),
-        ]
+        outs = outs + [shape((1536, 128), BF16)] + EDGES
         scratch = scratch + [pltpu.VMEM((256, 384), BF16)]
     return call(
         update_kernel(last), outs, [VMEM] * 13, scratch, 500_000_000,
@@ -555,8 +557,7 @@
     pickt = (slots_range[:, None] == jnp.concatenate([flat, flat])[None, :]).astype(BF16)
 
     state = fluid_state
-    payload = pack_call()(state, send)[0]
-    edges = (state[:, 0], state[:, 7], state[:, :, 0:1], state[:, :, 15:16])
+    payload, *edges = pack_call()(state, send)
     start_disp = node_disp.reshape(3, 32, 128).transpose(1, 0, 2)
     start_vel = node_vel.reshape(3, 32, 128).transpose(1, 0, 2)
     for step in range(STEPS):

time: 160 us -> 160 us (level)
  starting transfers between devices: 80.3 us -> 82.6 us
    all_to_all x6, waiting for transfers between devices: 18.3 us -> 15.1 us  [exchange(): lax.all_to_all(payload.reshape((128,) + dims + (128,)), AXES, split_axis=...]
    all_to_all x6, starting transfers between devices: 45.2 us -> 48.3 us  [exchange(): lax.all_to_all(payload.reshape((128,) + dims + (128,)), AXES, split_axis=...]
    ppermute x12, waiting for transfers between devices: 14.6 us -> 16.7 us  [shift(): return (lax.ppermute(high, axis, up), lax.ppermute(low, axis, down))]
  transfers between devices with their start and end apart: 18 -> 18, of which waited for: 8 -> 6; matrix products, arithmetic and copies ran while one was open for 1% -> 1% of each run, Pallas kernels for 14% -> 9%
where the time goes in v3:
time: 160 us; the launch traced here: 159 us
  starting transfers between devices  82.6 us (52%)
  Pallas kernels  40.9 us (26%)
  waiting for transfers between devices  31.8 us (20%)
  other arithmetic  1.73 us (1%)
    all_to_all x6, starting transfers between devices, exchange(): lax.all_to_all(payload.reshape((128,) + dims + (128,)), AXES, split_axis=...  48.3 us
    ppermute x12, starting transfers between devices, shift(): return (lax.ppermute(high, axis, up), lax.ppermute(low, axis, down))  34.2 us
    pallas_call x3, Pallas kernels, body(): couple_call()  19.4 us
    ppermute x12, waiting for transfers between devices, shift(): return (lax.ppermute(high, axis, up), lax.ppermute(low, axis, down))  16.7 us
    all_to_all x6, waiting for transfers between devices, exchange(): lax.all_to_all(payload.reshape((128,) + dims + (128,)), AXES, split_axis=...  15.1 us
    pallas_call x2, Pallas kernels, body(): elastic_call(False)(displace, connectivity, share, *tables)  9.22 us
    pallas_call x1, Pallas kernels, body(): elastic_call(True)  5.83 us
    pallas_call x3, Pallas kernels, body(): update_call(last)  5.28 us
  transfers between devices with their start and end apart: 18, of which 6 were waited for; matrix products, arithmetic and copies ran while one was open for 1% of the time, Pallas kernels for 9%

profile of v3, /device:TPU:14, one launch (start us, length us, event | category | flops | bytes accessed | tf_op | source)
XLA Modules:
  0.0 159.1 jit_solution(16147995600378963846)
XLA Ops:
  0.6 0.7 select_bitcast_fusion
  1.3 0.1 fusion.send_ref
  1.5 0.0 copy-start
  1.5 1.0 copy-done
  2.5 1.1 shard_map.121
  3.6 10.4 %all-to-all-start = ((bf16[128,3,4,128]{3,2,1,0:T(4,128)(2,1)}), bf16[128,3,4,128]{3,2,1,0:T(4,128)(2,1)S(1)}, u32[]{:S(2)}, u32[]{:S(2)}) async-start(bf16[128,3,4,128]{3,2,1,0:T(4,128)(2,1)} %bitcast.3), calls=%async_computation | async-start | bytes 786432 | tf_op jit(solution)/shard_map/all_to_all | solution.py:523
  14.0 0.7 shift-right-arithmetic_add_fusion
  14.7 0.1 eq.62
  14.8 0.1 fusion.1.pickt_ref
  14.9 0.1 fusion.3.pick_ref
  15.0 5.8 %shard_map.122 = (f32[128,128]{1,0:T(8,128)S(1)}, f32[128,128]{1,0:T(8,128)S(1)}, f32[128,128]{1,0:T(8,128)S(1)}, f32[128,128]{1,0:T(8,128)S(1)}, f32[72,112]{1,...) custom-call(f32[32,3,128]{2,1,0:T(4,128)} %bitcast.45, f32[32,3,128]{2,1,0:T(4,128)} %bitcast.46, ...), custom_call_target="tpu_custom_call" | custom-call | flops 3000000000 | bytes 2000000 | tf_op jit(solution)/shard_map/pallas_call | solution.py:568
  20.8 0.0 copy-start.1
  20.8 0.0 copy-start.2
  20.8 3.6 %all-to-all-done = bf16[128,3,4,128]{3,2,1,0:T(4,128)(2,1)S(1)} async-done(((bf16[128,3,4,128]{3,2,1,0:T(4,128)(2,1)}), bf16[128,3,4,128]{3,2,1,0:T(4,128)(2,1)S(1)}, u32[]{:S(2)}, u32[]{:S(2)}) %all-to-all-start) | async-done | bytes 393248 | tf_op jit(solution)/shard_map/all_to_all | solution.py:523
  24.4 6.6 %shard_map.123 = (bf16[1792,128]{1,0:T(8,128)(2,1)}, f32[128,128]{1,0:T(8,128)S(1)}) custom-call(s32[4,32]{1,0:T(4,128)} %windex_ref.5, bf16[1536,128]{1,0:T(8,128)(2,1)S(1)} %bitcast.36, f32[128,128]{1,0:T(8,128)S(1)} %get-tuple-element.45.vel_ref, bf16[128,512]{1,0:T(8,128)(2,1)S(1)} %fusion.3.pick_ref, bf16[512,256]{1,0:T(8,128)(2,1)S(1)} %fusion.1.pickt_ref, ...), custom_call_target="tpu_custom_call" | custom-call | flops 1000000000 | bytes 2000000 | tf_op jit(solution)/shard_map/pallas_call | solution.py:573
  30.9 6.5 %all-to-all-start.1 = ((bf16[128,7,2,128]{3,2,1,0:T(2,128)(2,1)}), bf16[128,7,2,128]{3,2,1,0:T(2,128)(2,1)S(1)}, u32[]{:S(2)}, u32[]{:S(2)}) async-start(bf16[128,7,2,128]{3,2,1,0:T(2,128)(2,1)} %bitcast.11), calls=%async_computation.1 | async-start | bytes 917504 | tf_op jit(solution)/shard_map/all_to_all | solution.py:523
  37.5 2.0 %collective-permute-start = (bf16[4,16,256]{2,1,0:T(8,128)(2,1)S(1)}, bf16[4,16,256]{2,1,0:T(8,128)(2,1)S(1)}, u32[]{:S(2)}, u32[]{:S(2)}) collective-permute-start(bf16[4,16,256]{2,1,0:T(8,128)(2,1)S(1)} %get-tuple-element.48), channel_id=1, source_target_pairs={{0,16},{16,32},{32,48},{48,64},{64,80},{80,96},{96,112},{1,17},{17... | collective-permute-start | bytes 98312 | tf_op jit(solution)/shard_map/ppermute | solution.py:536
  39.5 3.5 %collective-permute-start.1 = (bf16[4,16,256]{2,1,0:T(8,128)(2,1)S(1)}, bf16[4,16,256]{2,1,0:T(8,128)(2,1)S(1)}, u32[]{:S(2)}, u32[]{:S(2)}) collective-permute-start(bf16[4,16,256]{2,1,0:T(8,128)(2,1)S(1)} %get-tuple-element.49), channel_id=1, source_target_pairs={{16,0},{32,16},{48,32},{64,48},{80,64},{96,80},{112,96},{17,1},{33... | collective-permute-start | bytes 98312 | tf_op jit(solution)/shard_map/ppermute | solution.py:536
  43.0 3.6 %collective-permute-start.2 = (f32[4,8,1,256]{3,2,1,0:T(1,128)S(1)}, f32[4,8,1,256]{3,2,1,0:T(1,128)S(1)}, u32[]{:S(2)}, u32[]{:S(2)}) collective-permute-start(f32[4,8,1,256]{3,2,1,0:T(1,128)S(1)} %get-tuple-element.50), channel_id=1, source_target_pairs={{0,1},{1,2},{2,3},{3,4},{4,5},{5,6},{6,7},{7,8},{8,9},{9,10},{10,1... | collective-permute-start | bytes 98312 | tf_op jit(solution)/shard_map/ppermute | solution.py:536
  46.6 2.3 %collective-permute-start.3 = (f32[4,8,1,256]{3,2,1,0:T(1,128)S(1)}, f32[4,8,1,256]{3,2,1,0:T(1,128)S(1)}, u32[]{:S(2)}, u32[]{:S(2)}) collective-permute-start(f32[4,8,1,256]{3,2,1,0:T(1,128)S(1)} %get-tuple-element.51), channel_id=1, source_target_pairs={{1,0},{2,1},{3,2},{4,3},{5,4},{6,5},{7,6},{8,7},{9,8},{10,9},{11,1... | collective-permute-start | bytes 98312 | tf_op jit(solution)/shard_map/ppermute | solution.py:536
  48.9 0.1 fusion.2.sendt_ref
  48.9 0.0 collective-permute-done.xlow_ref
  49.0 5.5 %collective-permute-done.3.yhigh_ref = f32[4,8,1,256]{3,2,1,0:T(1,128)S(1)} collective-permute-done((f32[4,8,1,256]{3,2,1,0:T(1,128)S(1)}, f32[4,8,1,256]{3,2,1,0:T(1,128)S(1)}, u32[]{:S(2)}, u32[]{:S(2)}) %collective-permute-start.3) | collective-permute-done | bytes 32800 | tf_op jit(solution)/shard_map/ppermute | solution.py:536
  54.5 1.9 %shard_map.124 = (f32[4,8,16,256]{3,2,1,0:T(8,128)S(1)}, f32[128,128]{1,0:T(8,128)S(1)}, f32[128,128]{1,0:T(8,128)S(1)}, bf16[1536,128]{1,0:T(8,128)(2,1)}, bf16...) custom-call(bf16[1792,128]{1,0:T(8,128)(2,1)S(1)} %bitcast.33, ...), custom_call_target="tpu_custom_call" | custom-call | flops 500000000 | bytes 2000000 | tf_op jit(solution)/shard_map/pallas_call | solution.py:577
  56.4 9.2 %all-to-all-start.2 = ((bf16[128,3,4,128]{3,2,1,0:T(4,128)(2,1)}), bf16[128,3,4,128]{3,2,1,0:T(4,128)(2,1)S(1)}, u32[]{:S(2)}, u32[]{:S(2)}) async-start(bf16[128,3,4,128]{3,2,1,0:T(4,128)(2,1)} %bitcast.15), calls=%async_computation.2 | async-start | bytes 786432 | tf_op jit(solution)/shard_map/all_to_all | solution.py:523
  65.6 4.6 %shard_map.125 = (f32[128,128]{1,0:T(8,128)S(1)}, f32[128,128]{1,0:T(8,128)S(1)}) custom-call(f32[128,128]{1,0:T(8,128)S(1)} %get-tuple-element.57.refs_0_.disp_ref, s32[27,512]{1,0:T(8,128)S(1)} %copy-done.3, s32[16,128]{1,0:T(8,128)S(1)} %bitcast.41, f32[72,112]{1,0:T(8,128)S(1)} %get-tuple-element.58.refs_3_, f32[112,72]{1,0:T(8,128)S(1)} %get-tuple-element.59.refs_4_, ...), custom_call_target="tpu_custom_call" | custom-call | flops 3000000000 | bytes 2000000 | tf_op jit(solution)/shard_map/pallas_call | solution.py:572
  70.3 5.7 %all-to-all-done.2 = bf16[128,3,4,128]{3,2,1,0:T(4,128)(2,1)S(1)} async-done(((bf16[128,3,4,128]{3,2,1,0:T(4,128)(2,1)}), bf16[128,3,4,128]{3,2,1,0:T(4,128)(2,1)S(1)}, u32[]{:S(2)}, u32[]{:S(2)}) %all-to-all-start.2) | async-done | bytes 393248 | tf_op jit(solution)/shard_map/all_to_all | solution.py:523
  76.0 6.4 %shard_map.126 = (bf16[1792,128]{1,0:T(8,128)(2,1)}, f32[128,128]{1,0:T(8,128)S(1)}) custom-call(s32[4,32]{1,0:T(4,128)} %windex_ref.5, bf16[1536,128]{1,0:T(8,128)(2,1)S(1)} %bitcast.38, f32[128,128]{1,0:T(8,128)S(1)} %get-tuple-element.56.vel_ref, bf16[128,512]{1,0:T(8,128)(2,1)S(1)} %fusion.3.pick_ref, bf16[512,256]{1,0:T(8,128)(2,1)S(1)} %fusion.1.pickt_ref, ...), custom_call_target="tpu_custom_call" | custom-call | flops 1000000000 | bytes 2000000 | tf_op jit(solution)/shard_map/pallas_call | solution.py:573
  82.4 6.5 %all-to-all-start.3 = ((bf16[128,7,2,128]{3,2,1,0:T(2,128)(2,1)}), bf16[128,7,2,128]{3,2,1,0:T(2,128)(2,1)S(1)}, u32[]{:S(2)}, u32[]{:S(2)}) async-start(bf16[128,7,2,128]{3,2,1,0:T(2,128)(2,1)} %bitcast.18), calls=%async_computation.3 | async-start | bytes 917504 | tf_op jit(solution)/shard_map/all_to_all | solution.py:523
  88.9 2.0 %collective-permute-start.4 = (bf16[4,16,256]{2,1,0:T(8,128)(2,1)S(1)}, bf16[4,16,256]{2,1,0:T(8,128)(2,1)S(1)}, u32[]{:S(2)}, u32[]{:S(2)}) collective-permute-start(bf16[4,16,256]{2,1,0:T(8,128)(2,1)S(1)} %get-tuple-element.64), channel_id=1, source_target_pairs={{0,16},{16,32},{32,48},{48,64},{64,80},{80,96},{96,112},{1,17},{17... | collective-permute-start | bytes 98312 | tf_op jit(solution)/shard_map/ppermute | solution.py:536
  91.0 3.5 %collective-permute-start.5 = (bf16[4,16,256]{2,1,0:T(8,128)(2,1)S(1)}, bf16[4,16,256]{2,1,0:T(8,128)(2,1)S(1)}, u32[]{:S(2)}, u32[]{:S(2)}) collective-permute-start(bf16[4,16,256]{2,1,0:T(8,128)(2,1)S(1)} %get-tuple-element.65), channel_id=1, source_target_pairs={{16,0},{32,16},{48,32},{64,48},{80,64},{96,80},{112,96},{17,1},{33... | collective-permute-start | bytes 98312 | tf_op jit(solution)/shard_map/ppermute | solution.py:536
  94.5 3.6 %collective-permute-start.6 = (f32[4,8,1,256]{3,2,1,0:T(1,128)S(1)}, f32[4,8,1,256]{3,2,1,0:T(1,128)S(1)}, u32[]{:S(2)}, u32[]{:S(2)}) collective-permute-start(f32[4,8,1,256]{3,2,1,0:T(1,128)S(1)} %get-tuple-element.66), channel_id=1, source_target_pairs={{0,1},{1,2},{2,3},{3,4},{4,5},{5,6},{6,7},{7,8},{8,9},{9,10},{10,1... | collective-permute-start | bytes 98312 | tf_op jit(solution)/shard_map/ppermute | solution.py:536
  98.1 2.3 %collective-permute-start.7 = (f32[4,8,1,256]{3,2,1,0:T(1,128)S(1)}, f32[4,8,1,256]{3,2,1,0:T(1,128)S(1)}, u32[]{:S(2)}, u32[]{:S(2)}) collective-permute-start(f32[4,8,1,256]{3,2,1,0:T(1,128)S(1)} %get-tuple-element.67), channel_id=1, source_target_pairs={{1,0},{2,1},{3,2},{4,3},{5,4},{6,5},{7,6},{8,7},{9,8},{10,9},{11,1... | collective-permute-start | bytes 98312 | tf_op jit(solution)/shard_map/ppermute | solution.py:536
  100.4 0.0 collective-permute-done.4.xlow_ref
  100.4 0.0 collective-permute-done.6.ylow_ref
  100.4 5.6 %collective-permute-done.7.yhigh_ref = f32[4,8,1,256]{3,2,1,0:T(1,128)S(1)} collective-permute-done((f32[4,8,1,256]{3,2,1,0:T(1,128)S(1)}, f32[4,8,1,256]{3,2,1,0:T(1,128)S(1)}, u32[]{:S(2)}, u32[]{:S(2)}) %collective-permute-start.7) | collective-permute-done | bytes 32800 | tf_op jit(solution)/shard_map/ppermute | solution.py:536
  106.0 1.9 %shard_map.127 = (f32[4,8,16,256]{3,2,1,0:T(8,128)S(1)}, f32[128,128]{1,0:T(8,128)S(1)}, f32[128,128]{1,0:T(8,128)S(1)}, bf16[1536,128]{1,0:T(8,128)(2,1)}, bf16...) custom-call(bf16[1792,128]{1,0:T(8,128)(2,1)S(1)} %bitcast.34, ...), custom_call_target="tpu_custom_call" | custom-call | flops 500000000 | bytes 2000000 | tf_op jit(solution)/shard_map/pallas_call | solution.py:577
  107.9 9.2 %all-to-all-start.4 = ((bf16[128,3,4,128]{3,2,1,0:T(4,128)(2,1)}), bf16[128,3,4,128]{3,2,1,0:T(4,128)(2,1)S(1)}, u32[]{:S(2)}, u32[]{:S(2)}) async-start(bf16[128,3,4,128]{3,2,1,0:T(4,128)(2,1)} %bitcast.20), calls=%async_computation.4 | async-start | bytes 786432 | tf_op jit(solution)/shard_map/all_to_all | solution.py:523
  117.1 4.6 %shard_map.128 = (f32[128,128]{1,0:T(8,128)S(1)}, f32[128,128]{1,0:T(8,128)S(1)}) custom-call(f32[128,128]{1,0:T(8,128)S(1)} %get-tuple-element.72.refs_0_.disp_ref, s32[27,512]{1,0:T(8,128)S(1)} %copy-done.3, s32[16,128]{1,0:T(8,128)S(1)} %bitcast.43, f32[72,112]{1,0:T(8,128)S(1)} %get-tuple-element.58.refs_3_, f32[112,72]{1,0:T(8,128)S(1)} %get-tuple-element.59.refs_4_, ...), custom_call_target="tpu_custom_call" | custom-call | flops 3000000000 | bytes 2000000 | tf_op jit(solution)/shard_map/pallas_call | solution.py:572
  121.7 5.8 %all-to-all-done.4 = bf16[128,3,4,128]{3,2,1,0:T(4,128)(2,1)S(1)} async-done(((bf16[128,3,4,128]{3,2,1,0:T(4,128)(2,1)}), bf16[128,3,4,128]{3,2,1,0:T(4,128)(2,1)S(1)}, u32[]{:S(2)}, u32[]{:S(2)}) %all-to-all-start.4) | async-done | bytes 393248 | tf_op jit(solution)/shard_map/all_to_all | solution.py:523
  127.5 6.4 %shard_map.129 = (bf16[1792,128]{1,0:T(8,128)(2,1)}, f32[128,128]{1,0:T(8,128)S(1)}) custom-call(s32[4,32]{1,0:T(4,128)} %windex_ref.5, bf16[1536,128]{1,0:T(8,128)(2,1)S(1)} %bitcast.37, f32[128,128]{1,0:T(8,128)S(1)} %get-tuple-element.71.vel_ref, bf16[128,512]{1,0:T(8,128)(2,1)S(1)} %fusion.3.pick_ref, bf16[512,256]{1,0:T(8,128)(2,1)S(1)} %fusion.1.pickt_ref, ...), custom_call_target="tpu_custom_call" | custom-call | flops 1000000000 | bytes 2000000 | tf_op jit(solution)/shard_map/pallas_call | solution.py:573
  133.9 6.5 %all-to-all-start.5 = ((bf16[128,7,2,128]{3,2,1,0:T(2,128)(2,1)}), bf16[128,7,2,128]{3,2,1,0:T(2,128)(2,1)S(1)}, u32[]{:S(2)}, u32[]{:S(2)}) async-start(bf16[128,7,2,128]{3,2,1,0:T(2,128)(2,1)} %bitcast.22), calls=%async_computation.5 | async-start | bytes 917504 | tf_op jit(solution)/shard_map/all_to_all | solution.py:523
  140.4 2.0 %collective-permute-start.8 = (bf16[4,16,256]{2,1,0:T(8,128)(2,1)S(1)}, bf16[4,16,256]{2,1,0:T(8,128)(2,1)S(1)}, u32[]{:S(2)}, u32[]{:S(2)}) collective-permute-start(bf16[4,16,256]{2,1,0:T(8,128)(2,1)S(1)} %get-tuple-element.76), channel_id=1, source_target_pairs={{0,16},{16,32},{32,48},{48,64},{64,80},{80,96},{96,112},{1,17},{17... | collective-permute-start | bytes 98312 | tf_op jit(solution)/shard_map/ppermute | solution.py:536
  142.5 3.5 %collective-permute-start.9 = (bf16[4,16,256]{2,1,0:T(8,128)(2,1)S(1)}, bf16[4,16,256]{2,1,0:T(8,128)(2,1)S(1)}, u32[]{:S(2)}, u32[]{:S(2)}) collective-permute-start(bf16[4,16,256]{2,1,0:T(8,128)(2,1)S(1)} %get-tuple-element.77), channel_id=1, source_target_pairs={{16,0},{32,16},{48,32},{64,48},{80,64},{96,80},{112,96},{17,1},{33... | collective-permute-start | bytes 98312 | tf_op jit(solution)/shard_map/ppermute | solution.py:536
  146.0 3.6 %collective-permute-start.10 = (f32[4,8,1,256]{3,2,1,0:T(1,128)S(1)}, f32[4,8,1,256]{3,2,1,0:T(1,128)S(1)}, u32[]{:S(2)}, u32[]{:S(2)}) collective-permute-start(f32[4,8,1,256]{3,2,1,0:T(1,128)S(1)} %get-tuple-element.78), channel_id=1, source_target_pairs={{0,1},{1,2},{2,3},{3,4},{4,5},{5,6},{6,7},{7,8},{8,9},{9,10},{10,1... | collective-permute-start | bytes 98312 | tf_op jit(solution)/shard_map/ppermute | solution.py:536
  149.6 2.3 %collective-permute-start.11 = (f32[4,8,1,256]{3,2,1,0:T(1,128)S(1)}, f32[4,8,1,256]{3,2,1,0:T(1,128)S(1)}, u32[]{:S(2)}, u32[]{:S(2)}) collective-permute-start(f32[4,8,1,256]{3,2,1,0:T(1,128)S(1)} %get-tuple-element.79), channel_id=1, source_target_pairs={{1,0},{2,1},{3,2},{4,3},{5,4},{6,5},{7,6},{8,7},{9,8},{10,9},{11,1... | collective-permute-start | bytes 98312 | tf_op jit(solution)/shard_map/ppermute | solution.py:536
  151.9 5.6 %collective-permute-done.11.yhigh_ref = f32[4,8,1,256]{3,2,1,0:T(1,128)S(1)} collective-permute-done((f32[4,8,1,256]{3,2,1,0:T(1,128)S(1)}, f32[4,8,1,256]{3,2,1,0:T(1,128)S(1)}, u32[]{:S(2)}, u32[]{:S(2)}) %collective-permute-start.11) | collective-permute-done | bytes 32800 | tf_op jit(solution)/shard_map/ppermute | solution.py:536
  157.5 1.6 shard_map.130
  (14 shorter events, 0.0 us)
Async XLA Ops:
  1.5 1.0 copy-start
  3.6 20.7 %all-to-all-start = ((bf16[128,3,4,128]{3,2,1,0:T(4,128)(2,1)}), bf16[128,3,4,128]{3,2,1,0:T(4,128)(2,1)S(1)}, u32[]{:S(2)}, u32[]{:S(2)}) async-start(bf16[128,3,4,128]{3,2,1,0:T(4,128)(2,1)} %bitcast.3), calls=%async_computation | async-start | bytes 786432 | tf_op jit(solution)/shard_map/all_to_all | solution.py:523
  20.8 33.7 %copy-start.1 = (f32[4,8,16,256]{3,2,1,0:T(8,128)S(1)}, f32[4,8,16,256]{3,2,1,0:T(8,128)}, u32[]{:S(2)}) copy-start(f32[4,8,16,256]{3,2,1,0:T(8,128)} %state_ref.3) | copy-start | bytes 1572868
  20.8 33.7 %copy-start.2 = (s32[1,128,16]{1,2,0:T(8,128)S(1)}, s32[1,128,16]{1,2,0:T(8,128)}, u32[]{:S(2)}) copy-start(s32[1,128,16]{1,2,0:T(8,128)} %param.18) | copy-start | bytes 24580
  24.4 41.3 %copy-start.3 = (s32[27,512]{1,0:T(8,128)S(1)}, s32[27,512]{1,0:T(8,128)}, u32[]{:S(2)}) copy-start(s32[27,512]{1,0:T(8,128)} %refs_1_.3) | copy-start | bytes 165892
  30.9 23.6 %all-to-all-start.1 = ((bf16[128,7,2,128]{3,2,1,0:T(2,128)(2,1)}), bf16[128,7,2,128]{3,2,1,0:T(2,128)(2,1)S(1)}, u32[]{:S(2)}, u32[]{:S(2)}) async-start(bf16[128,7,2,128]{3,2,1,0:T(2,128)(2,1)} %bitcast.11), calls=%async_computation.1 | async-start | bytes 917504 | tf_op jit(solution)/shard_map/all_to_all | solution.py:523
  37.5 11.5 %collective-permute-start = (bf16[4,16,256]{2,1,0:T(8,128)(2,1)S(1)}, bf16[4,16,256]{2,1,0:T(8,128)(2,1)S(1)}, u32[]{:S(2)}, u32[]{:S(2)}) collective-permute-start(bf16[4,16,256]{2,1,0:T(8,128)(2,1)S(1)} %get-tuple-element.48), channel_id=1, source_target_pairs={{0,16},{16,32},{32,48},{48,64},{64,80},{80,96},{96,112},{1,17},{17... | collective-permute-start | bytes 98312 | tf_op jit(solution)/shard_map/ppermute | solution.py:536
  39.5 9.5 %collective-permute-start.1 = (bf16[4,16,256]{2,1,0:T(8,128)(2,1)S(1)}, bf16[4,16,256]{2,1,0:T(8,128)(2,1)S(1)}, u32[]{:S(2)}, u32[]{:S(2)}) collective-permute-start(bf16[4,16,256]{2,1,0:T(8,128)(2,1)S(1)} %get-tuple-element.49), channel_id=1, source_target_pairs={{16,0},{32,16},{48,32},{64,48},{80,64},{96,80},{112,96},{17,1},{33... | collective-permute-start | bytes 98312 | tf_op jit(solution)/shard_map/ppermute | solution.py:536
  43.0 5.9 %collective-permute-start.2 = (f32[4,8,1,256]{3,2,1,0:T(1,128)S(1)}, f32[4,8,1,256]{3,2,1,0:T(1,128)S(1)}, u32[]{:S(2)}, u32[]{:S(2)}) collective-permute-start(f32[4,8,1,256]{3,2,1,0:T(1,128)S(1)} %get-tuple-element.50), channel_id=1, source_target_pairs={{0,1},{1,2},{2,3},{3,4},{4,5},{5,6},{6,7},{7,8},{8,9},{9,10},{10,1... | collective-permute-start | bytes 98312 | tf_op jit(solution)/shard_map/ppermute | solution.py:536
  46.6 7.9 %collective-permute-start.3 = (f32[4,8,1,256]{3,2,1,0:T(1,128)S(1)}, f32[4,8,1,256]{3,2,1,0:T(1,128)S(1)}, u32[]{:S(2)}, u32[]{:S(2)}) collective-permute-start(f32[4,8,1,256]{3,2,1,0:T(1,128)S(1)} %get-tuple-element.51), channel_id=1, source_target_pairs={{1,0},{2,1},{3,2},{4,3},{5,4},{6,5},{7,6},{8,7},{9,8},{10,9},{11,1... | collective-permute-start | bytes 98312 | tf_op jit(solution)/shard_map/ppermute | solution.py:536
  56.4 19.6 %all-to-all-start.2 = ((bf16[128,3,4,128]{3,2,1,0:T(4,128)(2,1)}), bf16[128,3,4,128]{3,2,1,0:T(4,128)(2,1)S(1)}, u32[]{:S(2)}, u32[]{:S(2)}) async-start(bf16[128,3,4,128]{3,2,1,0:T(4,128)(2,1)} %bitcast.15), calls=%async_computation.2 | async-start | bytes 786432 | tf_op jit(solution)/shard_map/all_to_all | solution.py:523
  82.4 23.6 %all-to-all-start.3 = ((bf16[128,7,2,128]{3,2,1,0:T(2,128)(2,1)}), bf16[128,7,2,128]{3,2,1,0:T(2,128)(2,1)S(1)}, u32[]{:S(2)}, u32[]{:S(2)}) async-start(bf16[128,7,2,128]{3,2,1,0:T(2,128)(2,1)} %bitcast.18), calls=%async_computation.3 | async-start | bytes 917504 | tf_op jit(solution)/shard_map/all_to_all | solution.py:523
  88.9 11.4 %collective-permute-start.4 = (bf16[4,16,256]{2,1,0:T(8,128)(2,1)S(1)}, bf16[4,16,256]{2,1,0:T(8,128)(2,1)S(1)}, u32[]{:S(2)}, u32[]{:S(2)}) collective-permute-start(bf16[4,16,256]{2,1,0:T(8,128)(2,1)S(1)} %get-tuple-element.64), channel_id=1, source_target_pairs={{0,16},{16,32},{32,48},{48,64},{64,80},{80,96},{96,112},{1,17},{17... | collective-permute-start | bytes 98312 | tf_op jit(solution)/shard_map/ppermute | solution.py:536
  91.0 9.4 %collective-permute-start.5 = (bf16[4,16,256]{2,1,0:T(8,128)(2,1)S(1)}, bf16[4,16,256]{2,1,0:T(8,128)(2,1)S(1)}, u32[]{:S(2)}, u32[]{:S(2)}) collective-permute-start(bf16[4,16,256]{2,1,0:T(8,128)(2,1)S(1)} %get-tuple-element.65), channel_id=1, source_target_pairs={{16,0},{32,16},{48,32},{64,48},{80,64},{96,80},{112,96},{17,1},{33... | collective-permute-start | bytes 98312 | tf_op jit(solution)/shard_map/ppermute | solution.py:536
  94.5 5.9 %collective-permute-start.6 = (f32[4,8,1,256]{3,2,1,0:T(1,128)S(1)}, f32[4,8,1,256]{3,2,1,0:T(1,128)S(1)}, u32[]{:S(2)}, u32[]{:S(2)}) collective-permute-start(f32[4,8,1,256]{3,2,1,0:T(1,128)S(1)} %get-tuple-element.66), channel_id=1, source_target_pairs={{0,1},{1,2},{2,3},{3,4},{4,5},{5,6},{6,7},{7,8},{8,9},{9,10},{10,1... | collective-permute-start | bytes 98312 | tf_op jit(solution)/shard_map/ppermute | solution.py:536
  98.1 7.9 %collective-permute-start.7 = (f32[4,8,1,256]{3,2,1,0:T(1,128)S(1)}, f32[4,8,1,256]{3,2,1,0:T(1,128)S(1)}, u32[]{:S(2)}, u32[]{:S(2)}) collective-permute-start(f32[4,8,1,256]{3,2,1,0:T(1,128)S(1)} %get-tuple-element.67), channel_id=1, source_target_pairs={{1,0},{2,1},{3,2},{4,3},{5,4},{6,5},{7,6},{8,7},{9,8},{10,9},{11,1... | collective-permute-start | bytes 98312 | tf_op jit(solution)/shard_map/ppermute | solution.py:536
  107.9 19.6 %all-to-all-start.4 = ((bf16[128,3,4,128]{3,2,1,0:T(4,128)(2,1)}), bf16[128,3,4,128]{3,2,1,0:T(4,128)(2,1)S(1)}, u32[]{:S(2)}, u32[]{:S(2)}) async-start(bf16[128,3,4,128]{3,2,1,0:T(4,128)(2,1)} %bitcast.20), calls=%async_computation.4 | async-start | bytes 786432 | tf_op jit(solution)/shard_map/all_to_all | solution.py:523
  133.9 23.6 %all-to-all-start.5 = ((bf16[128,7,2,128]{3,2,1,0:T(2,128)(2,1)}), bf16[128,7,2,128]{3,2,1,0:T(2,128)(2,1)S(1)}, u32[]{:S(2)}, u32[]{:S(2)}) async-start(bf16[128,7,2,128]{3,2,1,0:T(2,128)(2,1)} %bitcast.22), calls=%async_computation.5 | async-start | bytes 917504 | tf_op jit(solution)/shard_map/all_to_all | solution.py:523
  140.4 11.4 %collective-permute-start.8 = (bf16[4,16,256]{2,1,0:T(8,128)(2,1)S(1)}, bf16[4,16,256]{2,1,0:T(8,128)(2,1)S(1)}, u32[]{:S(2)}, u32[]{:S(2)}) collective-permute-start(bf16[4,16,256]{2,1,0:T(8,128)(2,1)S(1)} %get-tuple-element.76), channel_id=1, source_target_pairs={{0,16},{16,32},{32,48},{48,64},{64,80},{80,96},{96,112},{1,17},{17... | collective-permute-start | bytes 98312 | tf_op jit(solution)/shard_map/ppermute | solution.py:536
  142.5 9.4 %collective-permute-start.9 = (bf16[4,16,256]{2,1,0:T(8,128)(2,1)S(1)}, bf16[4,16,256]{2,1,0:T(8,128)(2,1)S(1)}, u32[]{:S(2)}, u32[]{:S(2)}) collective-permute-start(bf16[4,16,256]{2,1,0:T(8,128)(2,1)S(1)} %get-tuple-element.77), channel_id=1, source_target_pairs={{16,0},{32,16},{48,32},{64,48},{80,64},{96,80},{112,96},{17,1},{33... | collective-permute-start | bytes 98312 | tf_op jit(solution)/shard_map/ppermute | solution.py:536
  146.0 5.9 %collective-permute-start.10 = (f32[4,8,1,256]{3,2,1,0:T(1,128)S(1)}, f32[4,8,1,256]{3,2,1,0:T(1,128)S(1)}, u32[]{:S(2)}, u32[]{:S(2)}) collective-permute-start(f32[4,8,1,256]{3,2,1,0:T(1,128)S(1)} %get-tuple-element.78), channel_id=1, source_target_pairs={{0,1},{1,2},{2,3},{3,4},{4,5},{5,6},{6,7},{7,8},{8,9},{9,10},{10,1... | collective-permute-start | bytes 98312 | tf_op jit(solution)/shard_map/ppermute | solution.py:536
  149.6 7.9 %collective-permute-start.11 = (f32[4,8,1,256]{3,2,1,0:T(1,128)S(1)}, f32[4,8,1,256]{3,2,1,0:T(1,128)S(1)}, u32[]{:S(2)}, u32[]{:S(2)}) collective-permute-start(f32[4,8,1,256]{3,2,1,0:T(1,128)S(1)} %get-tuple-element.79), channel_id=1, source_target_pairs={{1,0},{2,1},{3,2},{4,3},{5,4},{6,5},{7,6},{8,7},{9,8},{10,9},{11,1... | collective-permute-start | bytes 98312 | tf_op jit(solution)/shard_map/ppermute | solution.py:536
